TPU v7x, 128 devices: a whole 4x4x4 slice. The times are simulated.
128 devices in a mesh: prow: 8 (over z_hi, y), pcol: 16 (over x, z_lo, core).
Axes of the slice: x: 4, y: 4, z: 4 (z_hi: 2, z_lo: 2; z = z_hi * 2 + z_lo), core: 2. Of those that a mesh axis runs over, the one named last changes fastest.
Arguments:
- panel_t: float32 [16, 256, 8192], P('pcol', None, 'prow'), may hold values from -0.0625 to 0.0625
- ancestor: float32 [8192, 8192], P('prow', 'pcol'), as said below
- structure: int32 [16, 32], replicated, may hold values 0 or 1
- diag_inv: float32 [16, 256, 256], P('pcol'), may hold values from -6 to 6
Outputs:
- inverse_panel: float32 [4096, 8192], P('pcol', 'prow')
- inverse_diag: float32 [16, 256, 256], P('pcol')
Inputs may be any that keep to these rules, and one draw needn't show every extreme that they name: ancestor is symmetric up to rounding.
All inputs are finite; a program needn't handle non-finite values.
Results may differ from a plain program's by a relative error of at most 0.00007.
Values sent between devices are 32-bit elements; how exact they have to be, the bound alone decides.
No kernel may reach another device: no remote copies, remote signals or barrier semaphores. Data moves between devices by JAX's collectives and lax.ppermute only.
A program may use at most 128 MiB of HBM per device.

v0:
```python
import jax
import jax.numpy as jnp
from jax import lax
from jax.sharding import PartitionSpec as P


def copy_for_each(array, axis):
    length = lax.axis_size(axis)
    return lax.all_to_all(
        jnp.broadcast_to(array[None], (length, *array.shape)), axis, 0, 0, tiled=True
    )


def of_everyone(array, axis):
    everything = copy_for_each(array, axis)
    return jnp.sum(everything, axis=0)


def local(panel_t, ancestor, structure, diag_inv):
    local_sn = panel_t.shape[0]
    width = panel_t.shape[1]
    row_span = panel_t.shape[2]
    row_blocks = row_span // width
    col_index = lax.axis_index("pcol")
    row_index = lax.axis_index("prow")
    mine = lax.dynamic_slice(
        structure, (col_index * local_sn, row_index * row_blocks), (local_sn, row_blocks)
    )
    masked = (
        panel_t.reshape(local_sn, width, row_blocks, width)
        * mine.astype(jnp.float32)[:, None, :, None]
    )
    masked = masked.reshape(local_sn, width, row_span)
    prow_size = lax.axis_size("prow")
    rows_here = width // prow_size
    arranged = masked.reshape(local_sn, prow_size, rows_here, row_span).transpose(1, 0, 2, 3)
    gathered = lax.all_gather(arranged, "pcol", axis=1, tiled=True)
    total_nodes = gathered.shape[1]
    flat_rows = gathered.reshape(prow_size * total_nodes * rows_here, row_span)
    reduced = lax.psum_scatter(
        jnp.dot(
            flat_rows, ancestor, precision=lax.Precision.HIGHEST, preferred_element_type=jnp.float32
        ),
        "prow",
        scatter_dimension=0,
        tiled=True,
    )
    moved = lax.all_to_all(
        lax.all_to_all(reduced, "pcol", split_axis=0, concat_axis=1, tiled=True),
        "prow",
        split_axis=1,
        concat_axis=0,
        tiled=True,
    )
    summed = moved.reshape(prow_size, local_sn, rows_here, row_span).transpose(1, 0, 2, 3)
    summed = summed.reshape(local_sn * width, row_span)
    inverse_panel = -summed
    blocks = inverse_panel.reshape(local_sn, width, row_span)
    partial_diag = jnp.einsum("kbj,kcj->kbc", blocks, masked, precision=lax.Precision.HIGHEST)
    inverse_diag = diag_inv - of_everyone(partial_diag, "prow")
    return (inverse_panel, inverse_diag)


def solution(mesh):
    return jax.shard_map(
        local,
        mesh=mesh,
        in_specs=(P("pcol", None, "prow"), P("prow", "pcol"), P(), P("pcol", None, None)),
        out_specs=(P("pcol", "prow"), P("pcol", None, None)),
        check_vma=False,
    )
```

profile of v0, /device:TPU:32, one launch (start us, length us, event | category | flops | bytes accessed | tf_op | source)
XLA Modules:
  0.0 340.1 jit_solution(9076834743426126464)
XLA Ops:
  7.2 0.0 copy-start
  7.2 0.0 all-gather.2.cloned.1.call-start
  7.2 0.9 convert_bitcast_fusion
  8.1 0.1 broadcast_bitcast_fusion
  8.2 2.3 broadcast_multiply_fusion
  10.6 0.0 all-gather.2.cloned.1.call-update
  10.6 0.0 reduce-scatter.2.cloned.1.call-start
  10.6 93.6 %all-gather.2.cloned.1.call-done = f32[8,16,32,1024]{3,2,1,0:T(8,128)} async-done(((f32[8,1,32,1024]{3,2,1,0:T(8,128)}), f32[8,16,32,1024]{3,2,1,0:T(8,128)}) %all-gather.2.cloned.1.call-update) | async-done | bytes 16777232 | tf_op jit(solution)/shard_map/all_gather | solution.py:37
  104.3 0.0 copy-done
  104.3 30.3 %fusion.4 = f32[4096,512]{1,0:T(8,128)} fusion(f32[4096,1024]{1,0:T(8,128)} %bitcast.27, f32[1024,512]{1,0:T(8,128)S(1)} %copy-done), kind=kOutput, calls=%fused_computation.8 | convolution fusion | flops 25769803776 | bytes 27262976 | tf_op jit(solution)/shard_map/dot_general | solution.py:41
  134.5 0.0 reduce-scatter.2.cloned.1.call-update
  134.6 0.0 copy-start.1
  134.6 114.6 %reduce-scatter.2.cloned.1.call-done = f32[512,512]{1,0:T(8,128)} async-done(((f32[4096,512]{1,0:T(8,128)}), f32[512,512]{1,0:T(8,128)}) %reduce-scatter.2.cloned.1.call-update) | async-done | bytes 1048592 | tf_op jit(solution)/shard_map/reduce_scatter | solution.py:40
  249.1 20.5 %all_to_all.34 = f32[16,32,512]{2,1,0:T(8,128)S(1)} all-to-all(f32[16,32,512]{2,1,0:T(8,128)} %bitcast.24), channel_id=1, replica_groups=mesh['prow'=8,'pcol'=16] {'pcol'}, dimensions={0} | all-to-all | bytes 2097152 | tf_op jit(solution)/shard_map/all_to_all | solution.py:49
  269.7 1.6 copy.11
  271.2 2.5 all_to_all.28
  273.8 0.0 copy-start.3
  273.8 1.9 copy.12
  275.6 21.0 %all_to_all.35 = f32[32,8,1024]{2,0,1:T(8,128)S(1)} all-to-all(f32[32,8,1024]{2,0,1:T(8,128)S(1)} %copy.12), channel_id=1, replica_groups=mesh['prow'=8,'pcol'=16] {'prow'}, dimensions={1} | all-to-all | bytes 2097152 | tf_op jit(solution)/shard_map/all_to_all | solution.py:48
  296.7 0.1 neg.13
  296.8 0.0 copy-start.2
  296.8 1.0 copy-done.2
  297.8 0.0 copy-done.1
  297.8 1.0 fusion
  298.8 0.2 broadcast_in_dim.2
  299.0 31.7 %all_to_all.36 = f32[8,1,256,256]{3,2,1,0:T(8,128)} all-to-all(f32[8,1,256,256]{3,2,1,0:T(8,128)S(1)} %broadcast_in_dim.2), channel_id=1, replica_groups=mesh['prow'=8,'pcol'=16] {'prow'}, dimensions={0} | all-to-all | bytes 4194304 | tf_op jit(solution)/shard_map/all_to_all | solution.py:9
  330.8 1.8 reduce_sum.11
  332.5 0.0 copy-done.3
  332.5 0.7 bitcast_subtract_fusion
  (1 shorter events, 0.0 us)
Async XLA Ops:
  7.2 97.1 %copy-start = (f32[1024,512]{1,0:T(8,128)S(1)}, f32[1024,512]{1,0:T(8,128)}, u32[]{:S(2)}) copy-start(f32[1024,512]{1,0:T(8,128)} %param.5) | copy-start | bytes 6291460
  7.2 97.1 %all-gather.2.cloned.1.call-start = ((), (), s32[]{:S(2)}) async-start(), calls=%async_computation.4 | async-start | bytes 17825792 | tf_op jit(solution)/shard_map/all_gather | solution.py:37
  10.6 238.6 %reduce-scatter.2.cloned.1.call-start = ((), (), s32[]{:S(2)}) async-start(), calls=%async_computation.5 | async-start | bytes 9437184 | tf_op jit(solution)/shard_map/reduce_scatter | solution.py:40
  134.6 163.2 %copy-start.1 = (f32[1,256,1024]{2,1,0:T(8,128)S(1)}, f32[1,256,1024]{2,1,0:T(8,128)}, u32[]{:S(2)}) copy-start(f32[1,256,1024]{2,1,0:T(8,128)} %param.4) | copy-start | bytes 3145732
  273.8 58.8 %copy-start.3 = (f32[1,256,256]{2,1,0:T(8,128)S(1)}, f32[1,256,256]{2,1,0:T(8,128)}, u32[]{:S(2)}) copy-start(f32[1,256,256]{2,1,0:T(8,128)} %param.7) | copy-start | bytes 786436
  296.8 1.0 copy-start.2
Sparse Core Ops, SparseCore 0:
  10.7 93.5 all-gather.1
  134.7 114.4 reduce-scatter.1
where the time goes:
time: 340 us
  waiting for transfers between devices  208 us (61%)
  blocking collectives  73.3 us (22%)
  matrix products  31.3 us (9%)
  between operations  14.1 us (4%)
  local copies, waits for them, and re-layouts  7.22 us (2%)
  other arithmetic  5.85 us (2%)
    reduce_scatter x1, waiting for transfers between devices, local(): lax.psum_scatter(jnp.dot(flat_rows, ancestor, precision=lax.Precision.HIG...  115 us
    all_gather x1, waiting for transfers between devices, local(): gathered = lax.all_gather(arranged, 'pcol', axis=1, tiled=True)  93.6 us
    all_to_all x1, blocking collectives, copy_for_each(): lax.all_to_all(jnp.broadcast_to(array[None], (length, *array.shape)), axi...  31.7 us
    dot_general x1, matrix products, local(): jnp.dot(flat_rows, ancestor, precision=lax.Precision.HIGHEST, preferred_e...  30.3 us
    all_to_all x1, blocking collectives, local(): lax.all_to_all(lax.all_to_all(reduced, 'pcol', split_axis=0, concat_axis=...  21 us
    all_to_all x1, blocking collectives, local(): lax.all_to_all(reduced, 'pcol', split_axis=0, concat_axis=1, tiled=True)  20.5 us
  transfers between devices with their start and end apart: 2, of which 2 were waited for; matrix products, arithmetic and copies ran while one was open for 0% of the time, Pallas kernels for 0%

commit v1 on v0

v1 whole, which is shorter than its diff:
```python
import jax
import jax.numpy as jnp
from jax import lax
from jax.experimental import pallas as pl
from jax.experimental.pallas import tpu as pltpu
from jax.sharding import PartitionSpec as P


AXES = ("prow", "pcol")
TILE = 256


def number(x, y, z, core):
    return ((z >> 1) * 4 + y) * 16 + x * 4 + (z & 1) * 2 + core


def pairs(on=None, off=None):
    found = []
    for x in range(4):
        for y in range(4):
            for z in range(4):
                move = on if (y & 1) == (z & 1) else off
                if move is not None:
                    for core in range(2):
                        tx, ty, tz, tc = move(x, y, z, core)
                        found.append((number(x, y, z, core), number(tx % 4, ty % 4, tz % 4, tc)))
    return found


def shift(dy, dz):
    return lambda x, y, z, c: (x, y + dy, z + dz, c)


def both(move):
    return pairs(move, move)


X_UP = both(lambda x, y, z, c: (x + 1, y, z, c))
X_DOWN = both(lambda x, y, z, c: (x - 1, y, z, c))
CORE = both(lambda x, y, z, c: (x, y, z, 1 - c))
Z_MATE = both(lambda x, y, z, c: (x, y, z ^ 1, c))
Z_FAR = both(shift(0, 2))
Y_BY = [None] + [both(shift(d, 0)) for d in (1, 2, 3)]
P_ROUTES = [
    pairs(off=shift(0, 1), on=shift(1, 0)),
    pairs(off=shift(0, -1), on=shift(1, 2)),
    pairs(off=shift(2, 1), on=shift(-1, 0)),
    pairs(off=shift(2, -1), on=shift(-1, 2)),
]
Q_ROUTES = [
    pairs(off=shift(1, 1)),
    pairs(off=shift(1, -1), on=shift(0, 2)),
    pairs(off=shift(-1, 1), on=shift(2, 0)),
    pairs(off=shift(-1, -1), on=shift(2, 2)),
]
TO_OFF_MATE = pairs(on=lambda x, y, z, c: (x, y, z ^ 1, c))


def send(array, route):
    return lax.ppermute(array, AXES, route)


def parts(value):
    high = value.astype(jnp.bfloat16)
    return high, (value - high.astype(jnp.float32)).astype(jnp.bfloat16)


def dot(a, b):
    return lax.dot_general(a, b, (((1,), (1,)), ((), ())), preferred_element_type=jnp.float32)


def multiply_kernel(place, x0, x1, x2, x3, *rest):
    pieces = rest[:8]
    out, high, low = rest[8:]
    half = x0.shape[1] // 2

    @pl.when(pl.program_id(0) == 0)
    def _():
        for slot, ref in enumerate((x0, x1, x2, x3)):
            for g in range(2):
                a, b = parts(ref[:, g * half : (g + 1) * half])
                at = place[slot] * 2 + (g ^ place[4])
                high[at] = a
                low[at] = b

    acc = jnp.zeros(out.shape, jnp.float32)
    for j in range(8):
        a, b = parts(pieces[j][...])
        acc += dot(high[j], a) + dot(high[j], b) + dot(low[j], a)
    out[...] = acc


def multiply(place, slots, pieces):
    rows, span = slots[0].shape
    half = span // 2
    count = pieces[0].shape[0]
    whole = pl.BlockSpec((rows, span), lambda i, place: (0, 0))
    tile = pl.BlockSpec((TILE, half), lambda i, place: (i, 0))
    return pl.pallas_call(
        multiply_kernel,
        grid_spec=pltpu.PrefetchScalarGridSpec(
            num_scalar_prefetch=1,
            grid=(count // TILE,),
            in_specs=[whole] * 4 + [tile] * 8,
            out_specs=pl.BlockSpec((rows, TILE), lambda i, place: (0, i)),
            scratch_shapes=[pltpu.VMEM((8, rows, half), jnp.bfloat16)] * 2,
        ),
        out_shape=jax.ShapeDtypeStruct((rows, count), jnp.float32),
        compiler_params=pltpu.CompilerParams(vmem_limit_bytes=40 * 2**20),
        cost_estimate=pl.CostEstimate(
            flops=6 * rows * span * 4 * count, bytes_accessed=4 * (rows * span * 5 + span * 4 * count), transcendentals=0
        ),
    )(place, *slots, *pieces)


def product(left, right):
    return lax.dot_general(
        left,
        right,
        (((1,), (1,)), ((), ())),
        precision=lax.Precision.HIGH,
        preferred_element_type=jnp.float32,
    )


def local(panel_t, ancestor, structure, diag_inv):
    width = panel_t.shape[1]
    span = panel_t.shape[2]
    row_blocks = span // width
    prow = lax.axis_index("prow")
    pcol = lax.axis_index("pcol")
    x = pcol // 4
    y = prow & 3
    z = (prow >> 2) * 2 + ((pcol >> 1) & 1)
    core = pcol & 1
    on = (y & 1) == (z & 1)
    mine = lax.dynamic_slice(structure, (pcol, prow * row_blocks), (1, row_blocks))
    masked = panel_t.reshape(width, row_blocks, width) * mine.astype(jnp.float32).reshape(1, row_blocks, 1)
    own = masked.reshape(width, span)

    half = ancestor.shape[0] // 2
    left = send(ancestor, X_UP)
    right = send(ancestor, X_DOWN)
    p_slots = [send(own, route) for route in P_ROUTES]
    q_slots = [send(own, route) for route in Q_ROUTES]
    to_off = send(own, TO_OFF_MATE)
    far = jnp.concatenate([send(left[:half], X_UP), send(right[half:], X_DOWN)], axis=0)
    here = [ancestor, left, right, far]
    there = [send(piece, CORE) for piece in here]
    pieces = [piece for pair in zip(here, there) for piece in pair]

    first_y = jnp.where(on, y, (y + 3) & 3)
    p_high = jnp.where(on, ((z + 3) & 3) >> 1, z >> 1)
    q_high = jnp.where(on, z >> 1, ((z + 3) & 3) >> 1)

    def places(high):
        found = []
        for a in range(2):
            for r in range(2):
                block = (high ^ r) * 2 + ((first_y >> 1) ^ a)
                delta = (block - x) & 3
                found.append(jnp.where(delta == 0, 0, jnp.where(delta == 3, 1, delta + 1)))
        return jnp.stack(found + [core] + [core] * 3).astype(jnp.int32)

    q_slots[0] = jnp.where(on, own, q_slots[0])
    p_out = multiply(places(p_high), p_slots, pieces)
    q_out = multiply(places(q_high), q_slots, pieces)
    mate_out = jnp.where(on, p_out, q_out)
    own_out = jnp.where(on, q_out, p_out)

    mate_panel = jnp.where(on, jnp.where((z & 1) == 1, p_slots[0], p_slots[1]), to_off)
    mate_diag = send(product(mate_out, mate_panel), Z_MATE)
    inverse_panel = -(own_out + send(mate_out, Z_MATE))
    partial = product(own_out, own) + mate_diag

    quarter = width // 4
    cut = partial.reshape(4, quarter, width)
    summed = lax.dynamic_index_in_dim(cut, y, 0, False)
    for d in (1, 2, 3):
        summed = summed + send(lax.dynamic_index_in_dim(cut, (y + d) & 3, 0, False), Y_BY[d])
    summed = summed + send(summed, Z_FAR)
    diag = jnp.zeros((4, quarter, width), jnp.float32)
    diag = lax.dynamic_update_index_in_dim(diag, summed, y, 0)
    for d in (1, 2, 3):
        diag = lax.dynamic_update_index_in_dim(diag, send(summed, Y_BY[d]), (y - d) & 3, 0)
    return inverse_panel, diag_inv + diag.reshape(1, width, width)


def solution(mesh):
    return jax.shard_map(
        local,
        mesh=mesh,
        in_specs=(P("pcol", None, "prow"), P("prow", "pcol"), P(), P("pcol", None, None)),
        out_specs=(P("pcol", "prow"), P("pcol", None, None)),
        check_vma=False,
    )
```

time: 340 us -> 319 us (0.938)
  blocking collectives: 73.3 us -> 0 us
  starting transfers between devices: 0.08 us -> 43.1 us
  matrix products: 31.3 us -> 2.59 us
  Pallas kernels: 0 us -> 22.2 us
  between operations: 14.1 us -> 0.88 us
  local copies, waits for them, and re-layouts: 7.22 us -> 20.4 us
  waiting for transfers between devices: 208 us -> 218 us
  other arithmetic: 5.85 us -> 9.9 us
    ppermute x0 -> x26, waiting for transfers between devices: none -> 218 us  [send(): return lax.ppermute(array, AXES, route)]
    reduce_scatter x1 -> x0, waiting for transfers between devices: 115 us -> none  [local(): lax.psum_scatter(jnp.dot(flat_rows, ancestor, precision=lax.Precision.HIG...]
    all_gather x1 -> x0, waiting for transfers between devices: 93.6 us -> none  [local(): gathered = lax.all_gather(arranged, 'pcol', axis=1, tiled=True)]
    all_to_all x3 -> x0, blocking collectives: 73.3 us -> none  [the longest x1 31.7 us: copy_for_each(): lax.all_to_all(jnp.broadcast_to(array[None], (length, *array.shape)), axi...]
    ppermute x0 -> x26, starting transfers between devices: none -> 43.1 us  [send(): return lax.ppermute(array, AXES, route)]
    dot_general x2, matrix products: 31.3 us -> 2.59 us  [product(): lax.dot_general(left, right, (((1,), (1,)), ((), ())), precision=lax.Prec...]
    pallas_call x0 -> x2, Pallas kernels: none -> 22.2 us  [multiply(): pl.pallas_call(multiply_kernel, grid_spec=pltpu.PrefetchScalarGridSpec(nu...]
    unnamed x10 -> x43, local copies, waits for them, and re-layouts: 1.06 us -> 15.9 us
  transfers between devices with their start and end apart: 2 -> 26, of which waited for: 2 -> 15; matrix products, arithmetic and copies ran while one was open for 0% -> 4% of each run, Pallas kernels for 0% -> 7%
where the time goes in v1:
time: 319 us; the launch traced here: 317 us
  waiting for transfers between devices  218 us (68%)
  starting transfers between devices  43.1 us (14%)
  Pallas kernels  22.2 us (7%)
  local copies, waits for them, and re-layouts  20.4 us (6%)
  other arithmetic  9.9 us (3%)
    ppermute x26, waiting for transfers between devices, send(): return lax.ppermute(array, AXES, route)  218 us
    ppermute x26, starting transfers between devices, send(): return lax.ppermute(array, AXES, route)  43.1 us
    pallas_call x2, Pallas kernels, multiply(): pl.pallas_call(multiply_kernel, grid_spec=pltpu.PrefetchScalarGridSpec(nu...  22.2 us
    unnamed x43, local copies, waits for them, and re-layouts  15.9 us
  transfers between devices with their start and end apart: 26, of which 15 were waited for; matrix products, arithmetic and copies ran while one was open for 4% of the time, Pallas kernels for 7%

profile of v1, /device:TPU:32, one launch (start us, length us, event | category | flops | bytes accessed | tf_op | source)
XLA Modules:
  0.0 317.1 jit_solution(3202850331683311188)
XLA Ops:
  0.6 1.6 collective-permute-start.5
  2.2 1.7 collective-permute-start.7
  4.8 2.3 bitcast_multiply_fusion
  7.1 5.0 %collective-permute-start = (f32[256,1024]{1,0:T(8,128)}, f32[256,1024]{1,0:T(8,128)S(1)}, u32[]{:S(2)}, u32[]{:S(2)}) collective-permute-start(f32[256,1024]{1,0:T(8,128)} %bitcast_multiply_fusion), channel_id=1, source_target_pairs={{2,80},{3,81},{66,16},{67,17},{16,34},{17,35},{80,98},{81,99},{34,... | collective-permute-start | bytes 3145736 | tf_op jit(solution)/shard_map/ppermute | solution.py:60
  12.1 37.5 %collective-permute-done.5.rest_2_ = f32[1024,512]{1,0:T(8,128)} collective-permute-done((f32[1024,512]{1,0:T(8,128)}, f32[1024,512]{1,0:T(8,128)}, u32[]{:S(2)}, u32[]{:S(2)}) %collective-permute-start.5) | collective-permute-done | bytes 2097184 | tf_op jit(solution)/shard_map/ppermute | solution.py:60
  52.6 3.0 collective-permute-start.10
  56.7 3.2 %collective-permute-start.2 = (f32[256,1024]{1,0:T(8,128)}, f32[256,1024]{1,0:T(8,128)S(1)}, u32[]{:S(2)}, u32[]{:S(2)}) collective-permute-start(f32[256,1024]{1,0:T(8,128)} %bitcast_multiply_fusion), channel_id=1, source_target_pairs={{0,32},{1,33},{2,112},{3,113},{64,96},{65,97},{66,48},{67,49},{16,... | collective-permute-start | bytes 3145736 | tf_op jit(solution)/shard_map/ppermute | solution.py:60
  61.0 15.3 %collective-permute-done.9 = f32[512,512]{1,0:T(8,128)S(1)} collective-permute-done((f32[512,512]{1,0:T(8,128)S(1)}, f32[512,512]{1,0:T(8,128)S(1)}, u32[]{:S(2)}, u32[]{:S(2)}) %collective-permute-start.9) | collective-permute-done | bytes 1048608 | tf_op jit(solution)/shard_map/ppermute | solution.py:60
  78.9 25.4 %collective-permute-done.1.x1 = f32[256,1024]{1,0:T(8,128)S(1)} collective-permute-done((f32[256,1024]{1,0:T(8,128)}, f32[256,1024]{1,0:T(8,128)S(1)}, u32[]{:S(2)}, u32[]{:S(2)}) %collective-permute-start.1) | collective-permute-done | bytes 1048608 | tf_op jit(solution)/shard_map/ppermute | solution.py:60
  106.3 4.2 %collective-permute-start.3 = (f32[256,1024]{1,0:T(8,128)}, f32[256,1024]{1,0:T(8,128)S(1)}, u32[]{:S(2)}, u32[]{:S(2)}) collective-permute-start(f32[256,1024]{1,0:T(8,128)} %bitcast_multiply_fusion), channel_id=1, source_target_pairs={{0,96},{1,97},{2,48},{3,49},{64,32},{65,33},{66,112},{67,113},{16,... | collective-permute-start | bytes 3145736 | tf_op jit(solution)/shard_map/ppermute | solution.py:60
  110.5 44.3 %collective-permute-done.3.x3 = f32[256,1024]{1,0:T(8,128)S(1)} collective-permute-done((f32[256,1024]{1,0:T(8,128)}, f32[256,1024]{1,0:T(8,128)S(1)}, u32[]{:S(2)}, u32[]{:S(2)}) %collective-permute-start.3) | collective-permute-done | bytes 1048608 | tf_op jit(solution)/shard_map/ppermute | solution.py:60
  157.2 3.5 %collective-permute-start.13 = (f32[256,1024]{1,0:T(8,128)}, f32[256,1024]{1,0:T(8,128)S(1)}, u32[]{:S(2)}, u32[]{:S(2)}) collective-permute-start(f32[256,1024]{1,0:T(8,128)} %bitcast_multiply_fusion), channel_id=1, source_target_pairs={{0,80},{1,81},{2,0},{3,1},{64,16},{65,17},{66,64},{67,65},{16,82},... | collective-permute-start | bytes 3145736 | tf_op jit(solution)/shard_map/ppermute | solution.py:60
  162.0 3.4 %collective-permute-start.14 = (f32[256,1024]{1,0:T(8,128)}, f32[256,1024]{1,0:T(8,128)}, u32[]{:S(2)}, u32[]{:S(2)}) collective-permute-start(f32[256,1024]{1,0:T(8,128)} %bitcast_multiply_fusion), channel_id=1, source_target_pairs={{0,48},{1,49},{2,96},{3,97},{64,112},{65,113},{66,32},{67,33},{16,... | collective-permute-start | bytes 3145736 | tf_op jit(solution)/shard_map/ppermute | solution.py:60
  166.1 1.6 broadcast_select_fusion.2.x0
  169.0 1.6 copy-done.5
  170.6 1.6 copy-done.8
  174.7 10.7 %shard_map.59 = f32[256,1024]{1,0:T(8,128)S(1)} custom-call(s32[8]{0:T(128)S(1)} %stack.45.place, f32[256,1024]{1,0:T(8,128)S(1)} %broadcast_select_fusion.2.x0, f32[256,1024]{1,0:T(8,128)S(1)} %copy-done.11, f32[256,1024]{1,0:T(8,128)S(1)} %copy-done.13, f32[256,1024]{1,0:T(8,128)S(1)} %copy-done.15, f32[1024,512]{1,0:T(8,128)S(1)} %copy-done.3, ...), custom_call_target="tpu_custom_call" | custom-call | flops 6442450944 | bytes 22020096 | tf_op jit(solution)/shard_map/pallas_call | solution.py:99
  185.4 42.8 %collective-permute-done.12.x0 = f32[256,1024]{1,0:T(8,128)S(1)} collective-permute-done((f32[256,1024]{1,0:T(8,128)}, f32[256,1024]{1,0:T(8,128)S(1)}, u32[]{:S(2)}, u32[]{:S(2)}) %collective-permute-start.12) | collective-permute-done | bytes 1048608 | tf_op jit(solution)/shard_map/ppermute | solution.py:60
  228.2 26.9 %collective-permute-done.13.x1 = f32[256,1024]{1,0:T(8,128)S(1)} collective-permute-done((f32[256,1024]{1,0:T(8,128)}, f32[256,1024]{1,0:T(8,128)S(1)}, u32[]{:S(2)}, u32[]{:S(2)}) %collective-permute-start.13) | collective-permute-done | bytes 1048608 | tf_op jit(solution)/shard_map/ppermute | solution.py:60
  257.4 11.4 %shard_map.60 = f32[256,1024]{1,0:T(8,128)S(1)} custom-call(s32[8]{0:T(128)S(1)} %stack.50.place, f32[256,1024]{1,0:T(8,128)S(1)} %collective-permute-done.12.x0, f32[256,1024]{1,0:T(8,128)S(1)} %copy-done.1, f32[256,1024]{1,0:T(8,128)} %collective-permute-done.14.x2, f32[256,1024]{1,0:T(8,128)} %collective-permute-done.15.x3, f32[1024,512]{1,0:T(8,128)S(1)} %copy-done.3, ...), custom_call_target="tpu_custom_call" | custom-call | flops 6442450944 | bytes 22020096 | tf_op jit(solution)/shard_map/pallas_call | solution.py:99
  270.0 6.7 %collective-permute-done.18 = f32[256,256]{1,0:T(8,128)} collective-permute-done((f32[256,256]{1,0:T(8,128)S(1)}, f32[256,256]{1,0:T(8,128)}, u32[]{:S(2)}, u32[]{:S(2)}) %collective-permute-start.18) | collective-permute-done | bytes 262176 | tf_op jit(solution)/shard_map/ppermute | solution.py:60
  276.7 1.9 convolution_add_fusion
  279.3 1.6 collective-permute-start.19
  281.9 2.4 collective-permute-start.21
  287.7 2.7 collective-permute-start.22
  292.0 2.3 collective-permute-done.22
  294.3 1.6 collective-permute-start.23
  295.9 3.1 collective-permute-start.24
  299.9 2.1 collective-permute-done.24
  303.4 1.7 bitcast_add_fusion
  305.0 9.6 %collective-permute-done.16 = f32[256,1024]{1,0:T(8,128)} collective-permute-done((f32[256,1024]{1,0:T(8,128)S(1)}, f32[256,1024]{1,0:T(8,128)}, u32[]{:S(2)}, u32[]{:S(2)}) %collective-permute-start.16) | collective-permute-done | bytes 1048608 | tf_op jit(solution)/shard_map/ppermute | solution.py:60
  314.6 2.5 add_negate_fusion
  (85 shorter events, 30.9 us)
Async XLA Ops:
  0.6 49.0 %collective-permute-start.5 = (f32[1024,512]{1,0:T(8,128)}, f32[1024,512]{1,0:T(8,128)}, u32[]{:S(2)}, u32[]{:S(2)}) collective-permute-start(f32[1024,512]{1,0:T(8,128)} %rest_0_.3), channel_id=1, source_target_pairs={{0,4},{1,5},{2,6},{3,7},{64,68},{65,69},{66,70},{67,71},{16,20},{1... | collective-permute-start | bytes 6291464 | tf_op jit(solution)/shard_map/ppermute | solution.py:60
  2.2 49.1 %collective-permute-start.7 = (f32[1024,512]{1,0:T(8,128)}, f32[1024,512]{1,0:T(8,128)}, u32[]{:S(2)}, u32[]{:S(2)}) collective-permute-start(f32[1024,512]{1,0:T(8,128)} %rest_0_.3), channel_id=1, source_target_pairs={{0,12},{1,13},{2,14},{3,15},{64,76},{65,77},{66,78},{67,79},{16,28... | collective-permute-start | bytes 6291464 | tf_op jit(solution)/shard_map/ppermute | solution.py:60
  7.1 52.8 %copy-start.2 = (f32[1024,512]{1,0:T(8,128)S(1)}, f32[1024,512]{1,0:T(8,128)}, u32[]{:S(2)}) copy-start(f32[1024,512]{1,0:T(8,128)} %rest_0_.3) | copy-start | bytes 6291460
  7.1 52.8 %collective-permute-start = (f32[256,1024]{1,0:T(8,128)}, f32[256,1024]{1,0:T(8,128)S(1)}, u32[]{:S(2)}, u32[]{:S(2)}) collective-permute-start(f32[256,1024]{1,0:T(8,128)} %bitcast_multiply_fusion), channel_id=1, source_target_pairs={{2,80},{3,81},{66,16},{67,17},{16,34},{17,35},{80,98},{81,99},{34,... | collective-permute-start | bytes 3145736 | tf_op jit(solution)/shard_map/ppermute | solution.py:60
  50.9 25.3 %collective-permute-start.9 = (f32[512,512]{1,0:T(8,128)S(1)}, f32[512,512]{1,0:T(8,128)S(1)}, u32[]{:S(2)}, u32[]{:S(2)}) collective-permute-start(f32[512,512]{1,0:T(8,128)S(1)} %slice.8), channel_id=1, source_target_pairs={{0,4},{1,5},{2,6},{3,7},{64,68},{65,69},{66,70},{67,71},{16,20},{1... | collective-permute-start | bytes 3145736 | tf_op jit(solution)/shard_map/ppermute | solution.py:60
  52.5 113.5 %copy-start.18 = (f32[1,256,1024]{2,1,0:T(8,128)S(1)}, f32[1,256,1024]{2,1,0:T(8,128)}, u32[]{:S(2)}) copy-start(f32[1,256,1024]{2,1,0:T(8,128)} %param.4) | copy-start | bytes 3145732
  52.6 24.3 %collective-permute-start.10 = (f32[512,512]{1,0:T(8,128)S(1)}, f32[512,512]{1,0:T(8,128)S(1)}, u32[]{:S(2)}, u32[]{:S(2)}) collective-permute-start(f32[512,512]{1,0:T(8,128)S(1)} %slice.9), channel_id=1, source_target_pairs={{0,12},{1,13},{2,14},{3,15},{64,76},{65,77},{66,78},{67,79},{16,28... | collective-permute-start | bytes 3145736 | tf_op jit(solution)/shard_map/ppermute | solution.py:60
  55.6 48.8 %collective-permute-start.1 = (f32[256,1024]{1,0:T(8,128)}, f32[256,1024]{1,0:T(8,128)S(1)}, u32[]{:S(2)}, u32[]{:S(2)}) collective-permute-start(f32[256,1024]{1,0:T(8,128)} %bitcast_multiply_fusion), channel_id=1, source_target_pairs={{0,64},{1,65},{2,16},{3,17},{64,0},{65,1},{66,80},{67,81},{16,98},... | collective-permute-start | bytes 3145736 | tf_op jit(solution)/shard_map/ppermute | solution.py:60
  56.7 48.7 %collective-permute-start.2 = (f32[256,1024]{1,0:T(8,128)}, f32[256,1024]{1,0:T(8,128)S(1)}, u32[]{:S(2)}, u32[]{:S(2)}) collective-permute-start(f32[256,1024]{1,0:T(8,128)} %bitcast_multiply_fusion), channel_id=1, source_target_pairs={{0,32},{1,33},{2,112},{3,113},{64,96},{65,97},{66,48},{67,49},{16,... | collective-permute-start | bytes 3145736 | tf_op jit(solution)/shard_map/ppermute | solution.py:60
  60.0 95.9 %collective-permute-start.4 = (f32[1024,512]{1,0:T(8,128)S(1)}, f32[1024,512]{1,0:T(8,128)S(1)}, u32[]{:S(2)}, u32[]{:S(2)}) collective-permute-start(f32[1024,512]{1,0:T(8,128)S(1)} %copy-done.2), channel_id=1, source_target_pairs={{0,1},{1,0},{2,3},{3,2},{64,65},{65,64},{66,67},{67,66},{16,17},{1... | collective-permute-start | bytes 6291464 | tf_op jit(solution)/shard_map/ppermute | solution.py:60
  76.2 84.4 %collective-permute-start.6 = (f32[1024,512]{1,0:T(8,128)}, f32[1024,512]{1,0:T(8,128)S(1)}, u32[]{:S(2)}, u32[]{:S(2)}) collective-permute-start(f32[1024,512]{1,0:T(8,128)} %collective-permute-done.5.rest_2_), channel_id=1, source_target_pairs={{0,1},{1,0},{2,3},{3,2},{64,65},{65,64},{66,67},{67,66},{16,17},{1... | collective-permute-start | bytes 6291464 | tf_op jit(solution)/shard_map/ppermute | solution.py:60
  76.9 88.5 %collective-permute-start.8 = (f32[1024,512]{1,0:T(8,128)}, f32[1024,512]{1,0:T(8,128)}, u32[]{:S(2)}, u32[]{:S(2)}) collective-permute-start(f32[1024,512]{1,0:T(8,128)} %collective-permute-done.7.rest_4_), channel_id=1, source_target_pairs={{0,1},{1,0},{2,3},{3,2},{64,65},{65,64},{66,67},{67,66},{16,17},{1... | collective-permute-start | bytes 6291464 | tf_op jit(solution)/shard_map/ppermute | solution.py:60
  105.4 62.3 %collective-permute-start.11 = (f32[1024,512]{1,0:T(8,128)}, f32[1024,512]{1,0:T(8,128)}, u32[]{:S(2)}, u32[]{:S(2)}) collective-permute-start(f32[1024,512]{1,0:T(8,128)} %constant_dynamic-update-slice_fusion.rest_6_), channel_id=1, source_target_pairs={{0,1},{1,0},{2,3},{3,2},{64,65},{65,64},{66,67},{67,66},{16,17},{1... | collective-permute-start | bytes 6291464 | tf_op jit(solution)/shard_map/ppermute | solution.py:60
  106.3 48.5 %collective-permute-start.3 = (f32[256,1024]{1,0:T(8,128)}, f32[256,1024]{1,0:T(8,128)S(1)}, u32[]{:S(2)}, u32[]{:S(2)}) collective-permute-start(f32[256,1024]{1,0:T(8,128)} %bitcast_multiply_fusion), channel_id=1, source_target_pairs={{0,96},{1,97},{2,48},{3,49},{64,32},{65,33},{66,112},{67,113},{16,... | collective-permute-start | bytes 3145736 | tf_op jit(solution)/shard_map/ppermute | solution.py:60
  155.8 72.4 %collective-permute-start.12 = (f32[256,1024]{1,0:T(8,128)}, f32[256,1024]{1,0:T(8,128)S(1)}, u32[]{:S(2)}, u32[]{:S(2)}) collective-permute-start(f32[256,1024]{1,0:T(8,128)} %bitcast_multiply_fusion), channel_id=1, source_target_pairs={{0,16},{1,17},{2,64},{3,65},{64,80},{65,81},{66,0},{67,1},{16,18},... | collective-permute-start | bytes 3145736 | tf_op jit(solution)/shard_map/ppermute | solution.py:60
  157.2 98.0 %collective-permute-start.13 = (f32[256,1024]{1,0:T(8,128)}, f32[256,1024]{1,0:T(8,128)S(1)}, u32[]{:S(2)}, u32[]{:S(2)}) collective-permute-start(f32[256,1024]{1,0:T(8,128)} %bitcast_multiply_fusion), channel_id=1, source_target_pairs={{0,80},{1,81},{2,0},{3,1},{64,16},{65,17},{66,64},{67,65},{16,82},... | collective-permute-start | bytes 3145736 | tf_op jit(solution)/shard_map/ppermute | solution.py:60
  162.0 94.1 %collective-permute-start.14 = (f32[256,1024]{1,0:T(8,128)}, f32[256,1024]{1,0:T(8,128)}, u32[]{:S(2)}, u32[]{:S(2)}) collective-permute-start(f32[256,1024]{1,0:T(8,128)} %bitcast_multiply_fusion), channel_id=1, source_target_pairs={{0,48},{1,49},{2,96},{3,97},{64,112},{65,113},{66,32},{67,33},{16,... | collective-permute-start | bytes 3145736 | tf_op jit(solution)/shard_map/ppermute | solution.py:60
  165.4 90.7 %collective-permute-start.15 = (f32[256,1024]{1,0:T(8,128)}, f32[256,1024]{1,0:T(8,128)}, u32[]{:S(2)}, u32[]{:S(2)}) collective-permute-start(f32[256,1024]{1,0:T(8,128)} %bitcast_multiply_fusion), channel_id=1, source_target_pairs={{0,112},{1,113},{2,32},{3,33},{64,48},{65,49},{66,96},{67,97},{16,... | collective-permute-start | bytes 3145736 | tf_op jit(solution)/shard_map/ppermute | solution.py:60
  166.1 3.0 copy-start.11
  167.7 101.3 %collective-permute-start.17 = (f32[256,1024]{1,0:T(8,128)}, f32[256,1024]{1,0:T(8,128)S(1)}, u32[]{:S(2)}, u32[]{:S(2)}) collective-permute-start(f32[256,1024]{1,0:T(8,128)} %bitcast_multiply_fusion), channel_id=1, source_target_pairs={{0,2},{1,3},{64,66},{65,67},{18,16},{19,17},{82,80},{83,81},{32,34... | collective-permute-start | bytes 3145736 | tf_op jit(solution)/shard_map/ppermute | solution.py:60
  174.7 81.5 %copy-start.6 = (f32[1024,512]{1,0:T(8,128)S(1)}, f32[1024,512]{1,0:T(8,128)}, u32[]{:S(2)}) copy-start(f32[1024,512]{1,0:T(8,128)} %copy-done.4) | copy-start | bytes 6291460
  174.7 81.5 %copy-start.9 = (f32[1024,512]{1,0:T(8,128)S(1)}, f32[1024,512]{1,0:T(8,128)}, u32[]{:S(2)}) copy-start(f32[1024,512]{1,0:T(8,128)} %copy-done.7) | copy-start | bytes 6291460
  270.0 6.7 %collective-permute-start.18 = (f32[256,256]{1,0:T(8,128)S(1)}, f32[256,256]{1,0:T(8,128)}, u32[]{:S(2)}, u32[]{:S(2)}) collective-permute-start(f32[256,256]{1,0:T(8,128)S(1)} %fusion), channel_id=1, source_target_pairs={{0,2},{1,3},{2,0},{3,1},{64,66},{65,67},{66,64},{67,65},{16,18},{1... | collective-permute-start | bytes 786440 | tf_op jit(solution)/shard_map/ppermute | solution.py:60
  270.0 20.5 %copy-start.17 = (f32[256,1024]{1,0:T(8,128)S(1)}, f32[256,1024]{1,0:T(8,128)}, u32[]{:S(2)}) copy-start(f32[256,1024]{1,0:T(8,128)} %copy-done.16) | copy-start | bytes 3145732
  279.3 6.3 %collective-permute-start.19 = (f32[64,256]{1,0:T(8,128)}, f32[64,256]{1,0:T(8,128)S(1)}, u32[]{:S(2)}, u32[]{:S(2)}) collective-permute-start(f32[64,256]{1,0:T(8,128)} %get-tuple-element.4), channel_id=1, source_target_pairs={{0,16},{1,17},{2,18},{3,19},{64,80},{65,81},{66,82},{67,83},{16,32... | collective-permute-start | bytes 196616 | tf_op jit(solution)/shard_map/ppermute | solution.py:60
  280.9 6.0 %collective-permute-start.20 = (f32[64,256]{1,0:T(8,128)}, f32[64,256]{1,0:T(8,128)S(1)}, u32[]{:S(2)}, u32[]{:S(2)}) collective-permute-start(f32[64,256]{1,0:T(8,128)} %get-tuple-element.6), channel_id=1, source_target_pairs={{0,32},{1,33},{2,34},{3,35},{64,96},{65,97},{66,98},{67,99},{16,48... | collective-permute-start | bytes 196616 | tf_op jit(solution)/shard_map/ppermute | solution.py:60
  281.9 5.0 %collective-permute-start.21 = (f32[64,256]{1,0:T(8,128)}, f32[64,256]{1,0:T(8,128)}, u32[]{:S(2)}, u32[]{:S(2)}) collective-permute-start(f32[64,256]{1,0:T(8,128)} %get-tuple-element.5), channel_id=1, source_target_pairs={{0,48},{1,49},{2,50},{3,51},{64,112},{65,113},{66,114},{67,115},{1... | collective-permute-start | bytes 196616 | tf_op jit(solution)/shard_map/ppermute | solution.py:60
  287.7 6.6 %collective-permute-start.22 = (f32[64,256]{1,0:T(8,128)S(1)}, f32[64,256]{1,0:T(8,128)S(1)}, u32[]{:S(2)}, u32[]{:S(2)}) collective-permute-start(f32[64,256]{1,0:T(8,128)S(1)} %fusion.6), channel_id=1, source_target_pairs={{0,64},{1,65},{2,66},{3,67},{64,0},{65,1},{66,2},{67,3},{16,80},{1... | collective-permute-start | bytes 196616 | tf_op jit(solution)/shard_map/ppermute | solution.py:60
  290.5 24.1 %collective-permute-start.16 = (f32[256,1024]{1,0:T(8,128)S(1)}, f32[256,1024]{1,0:T(8,128)}, u32[]{:S(2)}, u32[]{:S(2)}) collective-permute-start(f32[256,1024]{1,0:T(8,128)S(1)} %copy-done.17), channel_id=1, source_target_pairs={{0,2},{1,3},{2,0},{3,1},{64,66},{65,67},{66,64},{67,65},{16,18},{1... | collective-permute-start | bytes 3145736 | tf_op jit(solution)/shard_map/ppermute | solution.py:60
  294.3 5.5 %collective-permute-start.23 = (f32[64,256]{1,0:T(8,128)S(1)}, f32[64,256]{1,0:T(8,128)S(1)}, u32[]{:S(2)}, u32[]{:S(2)}) collective-permute-start(f32[64,256]{1,0:T(8,128)S(1)} %get-tuple-element.3), channel_id=1, source_target_pairs={{0,16},{1,17},{2,18},{3,19},{64,80},{65,81},{66,82},{67,83},{16,32... | collective-permute-start | bytes 196616 | tf_op jit(solution)/shard_map/ppermute | solution.py:60
  295.9 6.1 %collective-permute-start.24 = (f32[64,256]{1,0:T(8,128)S(1)}, f32[64,256]{1,0:T(8,128)S(1)}, u32[]{:S(2)}, u32[]{:S(2)}) collective-permute-start(f32[64,256]{1,0:T(8,128)S(1)} %get-tuple-element.3), channel_id=1, source_target_pairs={{0,32},{1,33},{2,34},{3,35},{64,96},{65,97},{66,98},{67,99},{16,48... | collective-permute-start | bytes 196616 | tf_op jit(solution)/shard_map/ppermute | solution.py:60
  299.1 4.3 %collective-permute-start.25 = (f32[64,256]{1,0:T(8,128)S(1)}, f32[64,256]{1,0:T(8,128)S(1)}, u32[]{:S(2)}, u32[]{:S(2)}) collective-permute-start(f32[64,256]{1,0:T(8,128)S(1)} %get-tuple-element.3), channel_id=1, source_target_pairs={{0,48},{1,49},{2,50},{3,51},{64,112},{65,113},{66,114},{67,115},{1... | collective-permute-start | bytes 196616 | tf_op jit(solution)/shard_map/ppermute | solution.py:60
  (14 other events, 18.5 us)

commit v2 on v1

v2 whole, which is shorter than its diff:
```python
import jax
import jax.numpy as jnp
from jax import lax
from jax.experimental import pallas as pl
from jax.experimental.pallas import tpu as pltpu
from jax.sharding import PartitionSpec as P


AXES = ("prow", "pcol")
TILE = 256


def number(x, y, z, core):
    return ((z >> 1) * 4 + y) * 16 + x * 4 + (z & 1) * 2 + core


def pairs(on=None, off=None):
    found = []
    for x in range(4):
        for y in range(4):
            for z in range(4):
                move = on if (y & 1) == (z & 1) else off
                if move is not None:
                    for core in range(2):
                        tx, ty, tz, tc = move(x, y, z, core)
                        found.append((number(x, y, z, core), number(tx % 4, ty % 4, tz % 4, tc)))
    return found


def shift(dy, dz):
    return lambda x, y, z, c: (x, y + dy, z + dz, c)


def both(move):
    return pairs(move, move)


X_UP = both(lambda x, y, z, c: (x + 1, y, z, c))
X_DOWN = both(lambda x, y, z, c: (x - 1, y, z, c))
CORE = both(lambda x, y, z, c: (x, y, z, 1 - c))
Y_BY = [None] + [both(shift(d, 0)) for d in (1, 2, 3)]
Z_FLIP = [None] + [both(lambda x, y, z, c, d=d: (x, y, z ^ d, c)) for d in (1, 2, 3)]


def send(array, route):
    return lax.ppermute(array, AXES, route)


def parts(value):
    high = value.astype(jnp.bfloat16)
    return high, (value - high.astype(jnp.float32)).astype(jnp.bfloat16)


def dot(a, b):
    return lax.dot_general(a, b, (((1,), (1,)), ((), ())), preferred_element_type=jnp.float32)


SLOTS = [
    ((0, -1), (-1, 2)),
    ((0, 1), (1, 2)),
    ((2, -1), (1, -1)),
    ((2, 1), (1, 1)),
    ((0, 0), (-1, 0)),
    ((2, 0), (1, 0)),
    ((0, 2), (-1, -1)),
    ((2, 2), (-1, 1)),
]


def slot_info(where, structure, entry, blocks):
    x, y, z, core = where[0], where[1], where[2], where[3]
    on = (y & 1) == (z & 1)
    ys = (y + jnp.where(on, entry[0][0], entry[1][0])) & 3
    zs = (z + jnp.where(on, entry[0][1], entry[1][1])) & 3
    block = (zs >> 1) * 4 + ys
    delta = ((block >> 1) - x) & 3
    place = jnp.where(delta == 0, 0, jnp.where(delta == 3, 1, delta + 1))
    supernode = x * 4 + (zs & 1) * 2 + core
    return place, [structure[supernode, block * blocks + b].astype(jnp.float32) for b in range(blocks)]


def cut_panel(value, keeps, at, high, low):
    rows = high.shape[2]
    for b, keep in enumerate(keeps):
        hi, lo = parts(value(b) * keep)
        g, inner = divmod(b * rows, high.shape[3])
        high[at, g, :, inner : inner + rows] = hi
        low[at, g, :, inner : inner + rows] = lo


def cut_ancestor(core, pieces, high, low):
    first = pl.program_id(0) < pl.num_programs(0) // 2
    values = [pieces[0][...], pieces[1][...]]
    for at in range(2, len(pieces), 2):
        values.append(jnp.where(first, pieces[at][...], pieces[at + 1][...]))
    for j, value in enumerate(values):
        at = (j // 2) * 2 + (core ^ (j % 2))
        high[at], low[at] = parts(value)


def slot_product(at, place, xh, xl, ah, al):
    acc = None
    for g in range(2):
        a, b = ah[place * 2 + g], al[place * 2 + g]
        term = dot(xh[at, g], a) + dot(xh[at, g], b) + dot(xl[at, g], a)
        acc = term if acc is None else acc + term
    return acc


def early_kernel(where, structure, *refs):
    own, from_left, opposite, from_right, two_off, t0, s0, s1 = refs[:8]
    pieces = refs[8:22]
    own_out, mate_out, xh, xl, ah, al = refs[22:]
    rows, span = own.shape
    blocks = span // rows
    on = (where[1] & 1) == (where[2] & 1)
    infos = [slot_info(where, structure, SLOTS[i], blocks) for i in (0, 1, 4, 5, 6)]

    @pl.when(pl.program_id(0) == 0)
    def _():
        choices = [(s0, s0), (s1, s1), (own, from_left), (opposite, from_right), (two_off, t0)]
        for at, ((a, b), (_, keeps)) in enumerate(zip(choices, infos)):

            def value(i, a=a, b=b):
                part = slice(i * rows, (i + 1) * rows)
                return a[:, part] if a is b else jnp.where(on, a[:, part], b[:, part])

            cut_panel(value, keeps, at, xh, xl)

    cut_ancestor(where[3], pieces, ah, al)
    terms = [slot_product(at, place, xh, xl, ah, al) for at, (place, _) in enumerate(infos)]
    sides = terms[0] + terms[1]
    own_out[...] = terms[2] + terms[3] + jnp.where(on, terms[4], sides)
    mate_out[...] = jnp.where(on, sides, terms[4])


def late_kernel(where, structure, *refs):
    s2, s3, w_top, w_bottom, t1, own_in, mate_in, own, s0, s1 = refs[:10]
    pieces = refs[10:24]
    own_out, mate_out, diag, xh, xl, ah, al = refs[24:]
    rows, span = s2.shape
    blocks = span // rows
    step = pl.program_id(0)
    y, z, core = where[1], where[2], where[3]
    on = (y & 1) == (z & 1)
    infos = [slot_info(where, structure, SLOTS[i], blocks) for i in (2, 3, 7)]

    @pl.when(step == 0)
    def _():
        def last(i):
            part = slice(i * rows, (i + 1) * rows)
            return jnp.where(on, jnp.concatenate([w_top[:, part], w_bottom[:, part]], axis=0), t1[:, part])

        cut_panel(lambda i: s2[:, i * rows : (i + 1) * rows], infos[0][1], 0, xh, xl)
        cut_panel(lambda i: s3[:, i * rows : (i + 1) * rows], infos[1][1], 1, xh, xl)
        cut_panel(last, infos[2][1], 2, xh, xl)
        diag[...] = jnp.zeros(diag.shape, jnp.float32)

    cut_ancestor(core, pieces, ah, al)
    terms = [slot_product(at, place, xh, xl, ah, al) for at, (place, _) in enumerate(infos)]
    own_sum = own_in[...] + jnp.where(on, terms[2], 0.0)
    mate_sum = mate_in[...] + terms[0] + terms[1] + jnp.where(on, 0.0, terms[2])
    own_out[...] = own_sum
    mate_out[...] = mate_sum

    column = ((z >> 1) * 4 + y) * blocks + step
    supernode = where[0] * 4 + (z & 1) * 2 + core
    keep_own = structure[supernode, column].astype(jnp.float32)
    keep_mate = structure[supernode ^ 2, column].astype(jnp.float32)
    panels = (own[...] * keep_own, jnp.where((z & 1) == 1, s0[...], s1[...]) * keep_mate)
    for r, (result, panel) in enumerate(zip((own_sum, mate_sum), panels)):
        a, b = parts(result)
        c, d = parts(panel)
        diag[r] += dot(a, c) + dot(a, d) + dot(b, c)

    @pl.when(step == pl.num_programs(0) - 1)
    def _():
        total = diag[0]
        diag[0] = total + jnp.where(on, 0.0, total.T)
        diag[1] = jnp.where(on, diag[1], 0.0)


def piece_specs(count, half):
    middle = count // TILE // 2
    every = pl.BlockSpec((TILE, half), lambda i, *_: (i, 0))
    top = pl.BlockSpec((TILE, half), lambda i, *_: (jnp.minimum(i, middle - 1), 0))
    bottom = pl.BlockSpec((TILE, half), lambda i, *_: (jnp.maximum(i - middle, 0), 0))
    return [every, every] + [top, bottom] * 6


def run(kernel, where, structure, fixed, tiles, pieces, with_diag):
    rows, span = fixed[0].shape
    half = span // 2
    count = pieces[0].shape[0]
    at_column = pl.BlockSpec((rows, TILE), lambda i, *_: (0, i))
    specs = [pl.BlockSpec(a.shape, lambda i, *_: (0, 0)) for a in fixed] + [at_column] * len(tiles)
    out = jax.ShapeDtypeStruct((rows, count), jnp.float32)
    outs, out_specs = [out, out], [at_column, at_column]
    if with_diag:
        outs.append(jax.ShapeDtypeStruct((2, rows, rows), jnp.float32))
        out_specs.append(pl.BlockSpec((2, rows, rows), lambda i, *_: (0, 0, 0)))
    slots = 3 if with_diag else 5
    return pl.pallas_call(
        kernel,
        grid_spec=pltpu.PrefetchScalarGridSpec(
            num_scalar_prefetch=2,
            grid=(count // TILE,),
            in_specs=specs + piece_specs(count, half),
            out_specs=out_specs,
            scratch_shapes=[pltpu.VMEM((slots, 2, rows, half), jnp.bfloat16)] * 2
            + [pltpu.VMEM((8, TILE, half), jnp.bfloat16)] * 2,
        ),
        out_shape=outs,
        compiler_params=pltpu.CompilerParams(vmem_limit_bytes=56 * 2**20),
        cost_estimate=pl.CostEstimate(
            flops=6 * slots * rows * span * count, bytes_accessed=4 * (rows * span * 10 + span * 4 * count), transcendentals=0
        ),
    )(where, structure, *fixed, *tiles, *pieces)


def local(panel_t, ancestor, structure, diag_inv):
    width = panel_t.shape[1]
    span = panel_t.shape[2]
    prow = lax.axis_index("prow")
    pcol = lax.axis_index("pcol")
    x = pcol >> 2
    y = prow & 3
    z = (prow >> 2) * 2 + ((pcol >> 1) & 1)
    core = pcol & 1
    on = (y & 1) == (z & 1)
    own = panel_t.reshape(width, span)
    split = width // 2
    half = ancestor.shape[0] // 2
    top, bottom = ancestor[:half], ancestor[half:]

    from_left = send(own, both(shift(1, 0)))
    from_right = send(own, both(shift(-1, 0)))
    two_off = send(own, pairs(on=shift(0, 2)))
    opposite = jnp.concatenate(
        [send(from_left[:split], both(shift(1, 0))), send(from_right[split:], both(shift(-1, 0)))],
        axis=0,
    )
    turned = jnp.where(on, two_off, own)
    s0 = send(turned, pairs(on=shift(1, 0), off=shift(0, 1)))
    s1 = send(turned, pairs(on=shift(-1, 0), off=shift(0, -1)))
    t0 = send(from_left, pairs(on=shift(0, 1)))
    t1 = send(from_left, pairs(on=shift(0, -1)))
    crossed = jnp.where(on, from_right, opposite)
    s2 = send(crossed, pairs(on=shift(0, 1), off=shift(0, 1)))
    s3 = send(crossed, pairs(on=shift(0, -1), off=shift(0, -1)))
    w_top = send(s0[:split], pairs(off=shift(1, 0)))
    w_bottom = send(s1[split:], pairs(off=shift(-1, 0)))

    halves = [send(top, X_UP), send(bottom, X_UP), send(top, X_DOWN), send(bottom, X_DOWN)]
    halves += [send(halves[0], X_UP), send(halves[3], X_DOWN)]
    pieces = [ancestor, send(ancestor, CORE)]
    for i in range(0, 6, 2):
        pair = halves[i : i + 2]
        pieces += pair + [send(piece, CORE) for piece in pair]

    where = jnp.stack([x, y, z, core]).astype(jnp.int32)
    own_part, mate_part = run(
        early_kernel, where, structure, [own, from_left, opposite, from_right, two_off, t0, s0, s1], [], pieces, False
    )
    own_out, mate_out, partial = run(
        late_kernel,
        where,
        structure,
        [s2, s3, w_top, w_bottom, t1],
        [own_part, mate_part, own, s0, s1],
        pieces,
        True,
    )
    received = send(mate_out, Z_FLIP[1])

    quarter = width // 4
    cut = partial.reshape(2, 4, quarter, width)
    summed = lax.dynamic_index_in_dim(cut, y, 1, False)
    for d in (1, 2, 3):
        summed = summed + send(lax.dynamic_index_in_dim(cut, (y + d) & 3, 1, False), Y_BY[d])
    mine, mates = summed[0], summed[1]
    total = mine + send(mates, Z_FLIP[1]) + send(mine, Z_FLIP[2]) + send(mates, Z_FLIP[3])
    own_out, total = lax.optimization_barrier((own_out, total))
    diag = jnp.zeros((4, quarter, width), jnp.float32)
    diag = lax.dynamic_update_index_in_dim(diag, total, y, 0)
    for d in (1, 2, 3):
        diag = lax.dynamic_update_index_in_dim(diag, send(total, Y_BY[d]), (y - d) & 3, 0)
    return -(own_out + received), diag_inv + diag.reshape(1, width, width)


def solution(mesh):
    return jax.shard_map(
        local,
        mesh=mesh,
        in_specs=(P("pcol", None, "prow"), P("prow", "pcol"), P(), P("pcol", None, None)),
        out_specs=(P("pcol", "prow"), P("pcol", None, None)),
        check_vma=False,
    )
```

time: 319 us -> 215 us (0.67)
  waiting for transfers between devices: 218 us -> 108 us
  Pallas kernels: 22.2 us -> 42.5 us
  local copies, waits for them, and re-layouts: 20.4 us -> 10.8 us
  other arithmetic: 9.9 us -> 4.9 us
  starting transfers between devices: 43.1 us -> 46.9 us
    ppermute x26 -> x36, waiting for transfers between devices: 218 us -> 108 us  [send(): return lax.ppermute(array, AXES, route)]
    pallas_call x2, Pallas kernels: 22.2 us -> 42.5 us  [run(): pl.pallas_call(kernel, grid_spec=pltpu.PrefetchScalarGridSpec(num_scalar_...]
    unnamed x43 -> x33, local copies, waits for them, and re-layouts: 15.9 us -> 4.22 us
    ppermute x26 -> x36, starting transfers between devices: 43.1 us -> 46.9 us  [send(): return lax.ppermute(array, AXES, route)]
  transfers between devices with their start and end apart: 26 -> 36, of which waited for: 15 -> 16; matrix products, arithmetic and copies ran while one was open for 4% -> 4% of each run, Pallas kernels for 7% -> 11%
where the time goes in v2:
time: 215 us; the launch traced here: 214 us
  waiting for transfers between devices  108 us (50%)
  starting transfers between devices  46.9 us (22%)
  Pallas kernels  42.5 us (20%)
  local copies, waits for them, and re-layouts  10.8 us (5%)
  other arithmetic  4.9 us (2%)
    ppermute x36, waiting for transfers between devices, send(): return lax.ppermute(array, AXES, route)  108 us
    ppermute x36, starting transfers between devices, send(): return lax.ppermute(array, AXES, route)  46.9 us
    pallas_call x2, Pallas kernels, run(): pl.pallas_call(kernel, grid_spec=pltpu.PrefetchScalarGridSpec(num_scalar_...  42.5 us
  transfers between devices with their start and end apart: 36, of which 16 were waited for; matrix products, arithmetic and copies ran while one was open for 4% of the time, Pallas kernels for 11%

profile of v2, /device:TPU:32, one launch (start us, length us, event | category | flops | bytes accessed | tf_op | source)
XLA Modules:
  0.0 214.0 jit_solution(14046209930373147454)
XLA Ops:
  1.5 5.8 %collective-permute-start.1 = (f32[256,1024]{1,0:T(8,128)}, f32[256,1024]{1,0:T(8,128)}, u32[]{:S(2)}, u32[]{:S(2)}) collective-permute-start(f32[256,1024]{1,0:T(8,128)} %bitcast.37), channel_id=1, source_target_pairs={{0,16},{1,17},{2,18},{3,19},{64,80},{65,81},{66,82},{67,83},{16,32... | collective-permute-start | bytes 3145736 | tf_op jit(solution)/shard_map/ppermute | solution.py:46
  7.3 1.5 collective-permute-start
  8.8 3.1 %fusion.2 = (f32[512,512]{1,0:T(8,128)}, f32[512,512]{1,0:T(8,128)}) fusion(f32[1024,512]{1,0:T(8,128)} %refs_10_.1), kind=kLoop, calls=%fused_computation.20 | loop fusion | bytes 4194304 | tf_op jit(solution)/shard_map/slice | solution.py:234
  11.9 1.5 collective-permute-start.14
  13.4 1.7 collective-permute-start.19
  15.4 16.5 %collective-permute-done.1.refs_1_ = f32[256,1024]{1,0:T(8,128)} collective-permute-done((f32[256,1024]{1,0:T(8,128)}, f32[256,1024]{1,0:T(8,128)}, u32[]{:S(2)}, u32[]{:S(2)}) %collective-permute-start.1) | collective-permute-done | bytes 1048608 | tf_op jit(solution)/shard_map/ppermute | solution.py:46
  31.9 2.8 %collective-permute-start.18 = (f32[512,512]{1,0:T(8,128)}, f32[512,512]{1,0:T(8,128)}, u32[]{:S(2)}, u32[]{:S(2)}) collective-permute-start(f32[512,512]{1,0:T(8,128)} %get-tuple-element.17), channel_id=1, source_target_pairs={{0,12},{1,13},{2,14},{3,15},{64,76},{65,77},{66,78},{67,79},{16,28... | collective-permute-start | bytes 3145736 | tf_op jit(solution)/shard_map/ppermute | solution.py:46
  35.0 4.5 %collective-permute-done.14.refs_10_.refs_12_ = f32[512,512]{1,0:T(8,128)} collective-permute-done((f32[512,512]{1,0:T(8,128)}, f32[512,512]{1,0:T(8,128)}, u32[]{:S(2)}, u32[]{:S(2)}) %collective-permute-start.14) | collective-permute-done | bytes 1048608 | tf_op jit(solution)/shard_map/ppermute | solution.py:46
  43.4 18.5 %collective-permute-done.15.refs_11_.refs_13_ = f32[512,512]{1,0:T(8,128)} collective-permute-done((f32[512,512]{1,0:T(8,128)}, f32[512,512]{1,0:T(8,128)}, u32[]{:S(2)}, u32[]{:S(2)}) %collective-permute-start.15) | collective-permute-done | bytes 1048608 | tf_op jit(solution)/shard_map/ppermute | solution.py:46
  62.4 2.7 %collective-permute-start.3 = (f32[128,1024]{1,0:T(8,128)S(1)}, f32[128,1024]{1,0:T(8,128)S(1)}, u32[]{:S(2)}, u32[]{:S(2)}) collective-permute-start(f32[128,1024]{1,0:T(8,128)S(1)} %slice.33), channel_id=1, source_target_pairs={{0,48},{1,49},{2,50},{3,51},{64,112},{65,113},{66,114},{67,115},{1... | collective-permute-start | bytes 1572872 | tf_op jit(solution)/shard_map/ppermute | solution.py:46
  65.2 8.5 %collective-permute-done.2 = f32[128,1024]{1,0:T(8,128)S(1)} collective-permute-done((f32[128,1024]{1,0:T(8,128)S(1)}, f32[128,1024]{1,0:T(8,128)S(1)}, u32[]{:S(2)}, u32[]{:S(2)}) %collective-permute-start.2) | collective-permute-done | bytes 524320 | tf_op jit(solution)/shard_map/ppermute | solution.py:46
  73.7 1.5 collective-permute-start.23
  77.2 5.5 %collective-permute-done.22.refs_18_.refs_20_ = f32[512,512]{1,0:T(8,128)} collective-permute-done((f32[512,512]{1,0:T(8,128)}, f32[512,512]{1,0:T(8,128)}, u32[]{:S(2)}, u32[]{:S(2)}) %collective-permute-start.22) | collective-permute-done | bytes 1048608 | tf_op jit(solution)/shard_map/ppermute | solution.py:46
  82.7 12.3 %collective-permute-done.23.refs_19_.refs_21_ = f32[512,512]{1,0:T(8,128)} collective-permute-done((f32[512,512]{1,0:T(8,128)}, f32[512,512]{1,0:T(8,128)}, u32[]{:S(2)}, u32[]{:S(2)}) %collective-permute-start.23) | collective-permute-done | bytes 1048608 | tf_op jit(solution)/shard_map/ppermute | solution.py:46
  95.0 2.9 %collective-permute-done.12.refs_5_ = f32[256,1024]{1,0:T(8,128)S(1)} collective-permute-done((f32[256,1024]{1,0:T(8,128)}, f32[256,1024]{1,0:T(8,128)S(1)}, u32[]{:S(2)}, u32[]{:S(2)}) %collective-permute-start.12) | collective-permute-done | bytes 1048608 | tf_op jit(solution)/shard_map/ppermute | solution.py:46
  103.2 3.6 %collective-permute-start.4 = (f32[256,1024]{1,0:T(8,128)}, f32[256,1024]{1,0:T(8,128)}, u32[]{:S(2)}, u32[]{:S(2)}) collective-permute-start(f32[256,1024]{1,0:T(8,128)} %broadcast_select_fusion.1), channel_id=1, source_target_pairs={{0,2},{1,3},{2,64},{3,65},{64,66},{65,67},{66,0},{67,1},{16,18},{1... | collective-permute-start | bytes 3145736 | tf_op jit(solution)/shard_map/ppermute | solution.py:46
  106.8 1.3 copy-done.5
  109.6 4.0 %collective-permute-start.10 = (f32[128,1024]{1,0:T(8,128)S(1)}, f32[128,1024]{1,0:T(8,128)S(1)}, u32[]{:S(2)}, u32[]{:S(2)}) collective-permute-start(f32[128,1024]{1,0:T(8,128)S(1)} %slice.35), channel_id=1, source_target_pairs={{2,50},{3,51},{66,114},{67,115},{16,0},{17,1},{80,64},{81,65},{34,... | collective-permute-start | bytes 1572872 | tf_op jit(solution)/shard_map/ppermute | solution.py:46
  113.6 1.5 collective-permute-start.8
  115.1 22.5 %shard_map.59 = (f32[256,1024]{1,0:T(8,128)}, f32[256,1024]{1,0:T(8,128)}) custom-call(s32[4]{0:T(128)} %pad_add_fusion.where, s32[16,32]{1,0:T(8,128)} %structure.3, f32[256,1024]{1,0:T(8,128)} %bitcast.39, f32[256,1024]{1,0:T(8,128)} %collective-permute-done.1.refs_1_, f32[256,1024]{1,0:T(8,128)} %copy-done.2, f32[256,1024]{1,0:T(8,128)} %collective-permute-done.refs_3_, ...), custom_call_target="tpu_custom_call" | custom-call | flops 8053063680 | bytes 27262976 | tf_op jit(solution)/shard_map/pallas_call | solution.py:203
  137.7 14.2 %collective-permute-done.5.refs_1_ = f32[256,1024]{1,0:T(8,128)} collective-permute-done((f32[256,1024]{1,0:T(8,128)}, f32[256,1024]{1,0:T(8,128)}, u32[]{:S(2)}, u32[]{:S(2)}) %collective-permute-start.5) | collective-permute-done | bytes 1048608 | tf_op jit(solution)/shard_map/ppermute | solution.py:46
  152.9 20.0 %shard_map.60 = (f32[256,1024]{1,0:T(8,128)}, f32[256,1024]{1,0:T(8,128)}, f32[2,256,256]{2,1,0:T(8,128)}) custom-call(s32[4]{0:T(128)} %pad_add_fusion.where, s32[16,32]{1,0:T(8,128)} %structure.3, f32[256,1024]{1,0:T(8,128)} %collective-permute-done.4.refs_0_, f32[256,1024]{1,0:T(8,128)} %collective-permute-done.5.refs_1_, f32[128,1024]{1,0:T(8,128)} %copy-done.13, ...), custom_call_target="tpu_custom_call" | custom-call | flops 4831838208 | bytes 27262976 | tf_op jit(solution)/shard_map/pallas_call | solution.py:203
  174.2 1.7 collective-permute-start.27
  175.9 1.5 collective-permute-start.28
  177.4 5.7 %collective-permute-done.26 = f32[2,64,256]{2,1,0:T(8,128)S(1)} collective-permute-done((f32[2,64,256]{2,1,0:T(8,128)S(1)}, f32[2,64,256]{2,1,0:T(8,128)S(1)}, u32[]{:S(2)}, u32[]{:S(2)}) %collective-permute-start.26) | collective-permute-done | bytes 131104 | tf_op jit(solution)/shard_map/ppermute | solution.py:46
  185.1 1.5 collective-permute-start.30
  186.6 1.6 collective-permute-start.31
  188.2 1.6 collective-permute-start.32
  189.8 1.5 collective-permute-done.30
  192.0 3.3 %collective-permute-start.34 = (f32[64,256]{1,0:T(8,128)S(1)}, f32[64,256]{1,0:T(8,128)S(1)}, u32[]{:S(2)}, u32[]{:S(2)}) collective-permute-start(f32[64,256]{1,0:T(8,128)S(1)} %add_add_fusion), channel_id=1, source_target_pairs={{0,32},{1,33},{2,34},{3,35},{64,96},{65,97},{66,98},{67,99},{16,48... | collective-permute-start | bytes 196616 | tf_op jit(solution)/shard_map/ppermute | solution.py:46
  195.4 2.0 collective-permute-done.33
  200.3 12.5 %collective-permute-done.32 = f32[256,1024]{1,0:T(8,128)S(1)} collective-permute-done((f32[256,1024]{1,0:T(8,128)}, f32[256,1024]{1,0:T(8,128)S(1)}, u32[]{:S(2)}, u32[]{:S(2)}) %collective-permute-start.32) | collective-permute-done | bytes 1048608 | tf_op jit(solution)/shard_map/ppermute | solution.py:46
  (95 shorter events, 23.3 us)
Async XLA Ops:
  0.6 14.5 %collective-permute-start.6 = (f32[256,1024]{1,0:T(8,128)}, f32[256,1024]{1,0:T(8,128)S(1)}, u32[]{:S(2)}, u32[]{:S(2)}) collective-permute-start(f32[256,1024]{1,0:T(8,128)} %bitcast.36), channel_id=1, source_target_pairs={{0,64},{1,65},{64,0},{65,1},{18,82},{19,83},{82,18},{83,19},{32,96... | collective-permute-start | bytes 3145736 | tf_op jit(solution)/shard_map/ppermute | solution.py:46
  1.5 30.4 %collective-permute-start.1 = (f32[256,1024]{1,0:T(8,128)}, f32[256,1024]{1,0:T(8,128)}, u32[]{:S(2)}, u32[]{:S(2)}) collective-permute-start(f32[256,1024]{1,0:T(8,128)} %bitcast.37), channel_id=1, source_target_pairs={{0,16},{1,17},{2,18},{3,19},{64,80},{65,81},{66,82},{67,83},{16,32... | collective-permute-start | bytes 3145736 | tf_op jit(solution)/shard_map/ppermute | solution.py:46
  7.3 27.6 %collective-permute-start = (f32[256,1024]{1,0:T(8,128)}, f32[256,1024]{1,0:T(8,128)}, u32[]{:S(2)}, u32[]{:S(2)}) collective-permute-start(f32[256,1024]{1,0:T(8,128)} %bitcast.38), channel_id=1, source_target_pairs={{0,48},{1,49},{2,50},{3,51},{64,112},{65,113},{66,114},{67,115},{1... | collective-permute-start | bytes 3145736 | tf_op jit(solution)/shard_map/ppermute | solution.py:46
  11.9 27.6 %collective-permute-start.14 = (f32[512,512]{1,0:T(8,128)}, f32[512,512]{1,0:T(8,128)}, u32[]{:S(2)}, u32[]{:S(2)}) collective-permute-start(f32[512,512]{1,0:T(8,128)} %get-tuple-element.17), channel_id=1, source_target_pairs={{0,4},{1,5},{2,6},{3,7},{64,68},{65,69},{66,70},{67,71},{16,20},{1... | collective-permute-start | bytes 3145736 | tf_op jit(solution)/shard_map/ppermute | solution.py:46
  13.4 27.2 %collective-permute-start.19 = (f32[512,512]{1,0:T(8,128)}, f32[512,512]{1,0:T(8,128)}, u32[]{:S(2)}, u32[]{:S(2)}) collective-permute-start(f32[512,512]{1,0:T(8,128)} %get-tuple-element.16), channel_id=1, source_target_pairs={{0,12},{1,13},{2,14},{3,15},{64,76},{65,77},{66,78},{67,79},{16,28... | collective-permute-start | bytes 3145736 | tf_op jit(solution)/shard_map/ppermute | solution.py:46
  15.1 46.8 %collective-permute-start.15 = (f32[512,512]{1,0:T(8,128)}, f32[512,512]{1,0:T(8,128)}, u32[]{:S(2)}, u32[]{:S(2)}) collective-permute-start(f32[512,512]{1,0:T(8,128)} %get-tuple-element.16), channel_id=1, source_target_pairs={{0,4},{1,5},{2,6},{3,7},{64,68},{65,69},{66,70},{67,71},{16,20},{1... | collective-permute-start | bytes 3145736 | tf_op jit(solution)/shard_map/ppermute | solution.py:46
  31.9 30.5 %collective-permute-start.18 = (f32[512,512]{1,0:T(8,128)}, f32[512,512]{1,0:T(8,128)}, u32[]{:S(2)}, u32[]{:S(2)}) collective-permute-start(f32[512,512]{1,0:T(8,128)} %get-tuple-element.17), channel_id=1, source_target_pairs={{0,12},{1,13},{2,14},{3,15},{64,76},{65,77},{66,78},{67,79},{16,28... | collective-permute-start | bytes 3145736 | tf_op jit(solution)/shard_map/ppermute | solution.py:46
  34.9 41.6 %collective-permute-start.7 = (f32[256,1024]{1,0:T(8,128)S(1)}, f32[256,1024]{1,0:T(8,128)S(1)}, u32[]{:S(2)}, u32[]{:S(2)}) collective-permute-start(f32[256,1024]{1,0:T(8,128)S(1)} %broadcast_select_fusion), channel_id=1, source_target_pairs={{0,16},{1,17},{2,64},{3,65},{64,80},{65,81},{66,0},{67,1},{16,18},... | collective-permute-start | bytes 3145736 | tf_op jit(solution)/shard_map/ppermute | solution.py:46
  39.5 37.2 %collective-permute-start.9 = (f32[256,1024]{1,0:T(8,128)S(1)}, f32[256,1024]{1,0:T(8,128)S(1)}, u32[]{:S(2)}, u32[]{:S(2)}) collective-permute-start(f32[256,1024]{1,0:T(8,128)S(1)} %broadcast_select_fusion), channel_id=1, source_target_pairs={{0,48},{1,49},{2,0},{3,1},{64,112},{65,113},{66,64},{67,65},{16,82... | collective-permute-start | bytes 3145736 | tf_op jit(solution)/shard_map/ppermute | solution.py:46
  40.6 42.1 %collective-permute-start.22 = (f32[512,512]{1,0:T(8,128)}, f32[512,512]{1,0:T(8,128)}, u32[]{:S(2)}, u32[]{:S(2)}) collective-permute-start(f32[512,512]{1,0:T(8,128)} %collective-permute-done.14.refs_10_.refs_12_), channel_id=1, source_target_pairs={{0,4},{1,5},{2,6},{3,7},{64,68},{65,69},{66,70},{67,71},{16,20},{1... | collective-permute-start | bytes 3145736 | tf_op jit(solution)/shard_map/ppermute | solution.py:46
  61.9 11.8 %collective-permute-start.2 = (f32[128,1024]{1,0:T(8,128)S(1)}, f32[128,1024]{1,0:T(8,128)S(1)}, u32[]{:S(2)}, u32[]{:S(2)}) collective-permute-start(f32[128,1024]{1,0:T(8,128)S(1)} %slice.32), channel_id=1, source_target_pairs={{0,16},{1,17},{2,18},{3,19},{64,80},{65,81},{66,82},{67,83},{16,32... | collective-permute-start | bytes 1572872 | tf_op jit(solution)/shard_map/ppermute | solution.py:46
  62.4 12.8 %collective-permute-start.3 = (f32[128,1024]{1,0:T(8,128)S(1)}, f32[128,1024]{1,0:T(8,128)S(1)}, u32[]{:S(2)}, u32[]{:S(2)}) collective-permute-start(f32[128,1024]{1,0:T(8,128)S(1)} %slice.33), channel_id=1, source_target_pairs={{0,48},{1,49},{2,50},{3,51},{64,112},{65,113},{66,114},{67,115},{1... | collective-permute-start | bytes 1572872 | tf_op jit(solution)/shard_map/ppermute | solution.py:46
  73.7 21.3 %collective-permute-start.23 = (f32[512,512]{1,0:T(8,128)}, f32[512,512]{1,0:T(8,128)}, u32[]{:S(2)}, u32[]{:S(2)}) collective-permute-start(f32[512,512]{1,0:T(8,128)} %collective-permute-done.19.refs_15_.refs_17_), channel_id=1, source_target_pairs={{0,12},{1,13},{2,14},{3,15},{64,76},{65,77},{66,78},{67,79},{16,28... | collective-permute-start | bytes 3145736 | tf_op jit(solution)/shard_map/ppermute | solution.py:46
  75.2 22.7 %collective-permute-start.12 = (f32[256,1024]{1,0:T(8,128)}, f32[256,1024]{1,0:T(8,128)S(1)}, u32[]{:S(2)}, u32[]{:S(2)}) collective-permute-start(f32[256,1024]{1,0:T(8,128)} %collective-permute-done.1.refs_1_), channel_id=1, source_target_pairs={{0,2},{1,3},{64,66},{65,67},{18,80},{19,81},{82,16},{83,17},{32,34... | collective-permute-start | bytes 3145736 | tf_op jit(solution)/shard_map/ppermute | solution.py:46
  76.6 30.2 %collective-permute-start.13 = (f32[1024,512]{1,0:T(8,128)S(1)}, f32[1024,512]{1,0:T(8,128)S(1)}, u32[]{:S(2)}, u32[]{:S(2)}) collective-permute-start(f32[1024,512]{1,0:T(8,128)S(1)} %copy-done), channel_id=1, source_target_pairs={{0,1},{1,0},{2,3},{3,2},{64,65},{65,64},{66,67},{67,66},{16,17},{1... | collective-permute-start | bytes 6291464 | tf_op jit(solution)/shard_map/ppermute | solution.py:46
  76.7 21.3 %collective-permute-start.16 = (f32[512,512]{1,0:T(8,128)}, f32[512,512]{1,0:T(8,128)S(1)}, u32[]{:S(2)}, u32[]{:S(2)}) collective-permute-start(f32[512,512]{1,0:T(8,128)} %collective-permute-done.14.refs_10_.refs_12_), channel_id=1, source_target_pairs={{0,1},{1,0},{2,3},{3,2},{64,65},{65,64},{66,67},{67,66},{16,17},{1... | collective-permute-start | bytes 3145736 | tf_op jit(solution)/shard_map/ppermute | solution.py:46
  82.7 15.8 %collective-permute-start.21 = (f32[512,512]{1,0:T(8,128)}, f32[512,512]{1,0:T(8,128)S(1)}, u32[]{:S(2)}, u32[]{:S(2)}) collective-permute-start(f32[512,512]{1,0:T(8,128)} %collective-permute-done.19.refs_15_.refs_17_), channel_id=1, source_target_pairs={{0,1},{1,0},{2,3},{3,2},{64,65},{65,64},{66,67},{67,66},{16,17},{1... | collective-permute-start | bytes 3145736 | tf_op jit(solution)/shard_map/ppermute | solution.py:46
  95.0 6.8 %collective-permute-start.17 = (f32[512,512]{1,0:T(8,128)}, f32[512,512]{1,0:T(8,128)S(1)}, u32[]{:S(2)}, u32[]{:S(2)}) collective-permute-start(f32[512,512]{1,0:T(8,128)} %collective-permute-done.15.refs_11_.refs_13_), channel_id=1, source_target_pairs={{0,1},{1,0},{2,3},{3,2},{64,65},{65,64},{66,67},{67,66},{16,17},{1... | collective-permute-start | bytes 3145736 | tf_op jit(solution)/shard_map/ppermute | solution.py:46
  98.0 11.6 %collective-permute-start.24 = (f32[512,512]{1,0:T(8,128)}, f32[512,512]{1,0:T(8,128)}, u32[]{:S(2)}, u32[]{:S(2)}) collective-permute-start(f32[512,512]{1,0:T(8,128)} %collective-permute-done.22.refs_18_.refs_20_), channel_id=1, source_target_pairs={{0,1},{1,0},{2,3},{3,2},{64,65},{65,64},{66,67},{67,66},{16,17},{1... | collective-permute-start | bytes 3145736 | tf_op jit(solution)/shard_map/ppermute | solution.py:46
  100.3 13.3 %collective-permute-start.25 = (f32[512,512]{1,0:T(8,128)}, f32[512,512]{1,0:T(8,128)}, u32[]{:S(2)}, u32[]{:S(2)}) collective-permute-start(f32[512,512]{1,0:T(8,128)} %collective-permute-done.23.refs_19_.refs_21_), channel_id=1, source_target_pairs={{0,1},{1,0},{2,3},{3,2},{64,65},{65,64},{66,67},{67,66},{16,17},{1... | collective-permute-start | bytes 3145736 | tf_op jit(solution)/shard_map/ppermute | solution.py:46
  101.9 35.8 %collective-permute-start.11 = (f32[256,1024]{1,0:T(8,128)}, f32[256,1024]{1,0:T(8,128)}, u32[]{:S(2)}, u32[]{:S(2)}) collective-permute-start(f32[256,1024]{1,0:T(8,128)} %collective-permute-done.1.refs_1_), channel_id=1, source_target_pairs={{0,66},{1,67},{64,2},{65,3},{18,16},{19,17},{82,80},{83,81},{32,98... | collective-permute-start | bytes 3145736 | tf_op jit(solution)/shard_map/ppermute | solution.py:46
  103.2 34.5 %collective-permute-start.4 = (f32[256,1024]{1,0:T(8,128)}, f32[256,1024]{1,0:T(8,128)}, u32[]{:S(2)}, u32[]{:S(2)}) collective-permute-start(f32[256,1024]{1,0:T(8,128)} %broadcast_select_fusion.1), channel_id=1, source_target_pairs={{0,2},{1,3},{2,64},{3,65},{64,66},{65,67},{66,0},{67,1},{16,18},{1... | collective-permute-start | bytes 3145736 | tf_op jit(solution)/shard_map/ppermute | solution.py:46
  108.2 43.8 %collective-permute-start.5 = (f32[256,1024]{1,0:T(8,128)}, f32[256,1024]{1,0:T(8,128)}, u32[]{:S(2)}, u32[]{:S(2)}) collective-permute-start(f32[256,1024]{1,0:T(8,128)} %broadcast_select_fusion.1), channel_id=1, source_target_pairs={{0,66},{1,67},{2,0},{3,1},{64,2},{65,3},{66,64},{67,65},{16,82},{1... | collective-permute-start | bytes 3145736 | tf_op jit(solution)/shard_map/ppermute | solution.py:46
  109.6 42.4 %collective-permute-start.10 = (f32[128,1024]{1,0:T(8,128)S(1)}, f32[128,1024]{1,0:T(8,128)S(1)}, u32[]{:S(2)}, u32[]{:S(2)}) collective-permute-start(f32[128,1024]{1,0:T(8,128)S(1)} %slice.35), channel_id=1, source_target_pairs={{2,50},{3,51},{66,114},{67,115},{16,0},{17,1},{80,64},{81,65},{34,... | collective-permute-start | bytes 1572872 | tf_op jit(solution)/shard_map/ppermute | solution.py:46
  113.6 38.3 %collective-permute-start.8 = (f32[128,1024]{1,0:T(8,128)S(1)}, f32[128,1024]{1,0:T(8,128)S(1)}, u32[]{:S(2)}, u32[]{:S(2)}) collective-permute-start(f32[128,1024]{1,0:T(8,128)S(1)} %slice.34), channel_id=1, source_target_pairs={{2,18},{3,19},{66,82},{67,83},{16,32},{17,33},{80,96},{81,97},{34,... | collective-permute-start | bytes 1572872 | tf_op jit(solution)/shard_map/ppermute | solution.py:46
  174.1 9.0 %collective-permute-start.26 = (f32[2,64,256]{2,1,0:T(8,128)S(1)}, f32[2,64,256]{2,1,0:T(8,128)S(1)}, u32[]{:S(2)}, u32[]{:S(2)}) collective-permute-start(f32[2,64,256]{2,1,0:T(8,128)S(1)} %get-tuple-element.18), channel_id=1, source_target_pairs={{0,16},{1,17},{2,18},{3,19},{64,80},{65,81},{66,82},{67,83},{16,32... | collective-permute-start | bytes 393224 | tf_op jit(solution)/shard_map/ppermute | solution.py:46
  174.2 8.9 %collective-permute-start.27 = (f32[2,64,256]{2,1,0:T(8,128)S(1)}, f32[2,64,256]{2,1,0:T(8,128)S(1)}, u32[]{:S(2)}, u32[]{:S(2)}) collective-permute-start(f32[2,64,256]{2,1,0:T(8,128)S(1)} %get-tuple-element.20), channel_id=1, source_target_pairs={{0,32},{1,33},{2,34},{3,35},{64,96},{65,97},{66,98},{67,99},{16,48... | collective-permute-start | bytes 393224 | tf_op jit(solution)/shard_map/ppermute | solution.py:46
  175.9 7.8 %collective-permute-start.28 = (f32[2,64,256]{2,1,0:T(8,128)S(1)}, f32[2,64,256]{2,1,0:T(8,128)S(1)}, u32[]{:S(2)}, u32[]{:S(2)}) collective-permute-start(f32[2,64,256]{2,1,0:T(8,128)S(1)} %get-tuple-element.19), channel_id=1, source_target_pairs={{0,48},{1,49},{2,50},{3,51},{64,112},{65,113},{66,114},{67,115},{1... | collective-permute-start | bytes 393224 | tf_op jit(solution)/shard_map/ppermute | solution.py:46
  185.1 6.2 %collective-permute-start.30 = (f32[64,256]{1,0:T(8,128)S(1)}, f32[64,256]{1,0:T(8,128)S(1)}, u32[]{:S(2)}, u32[]{:S(2)}) collective-permute-start(f32[64,256]{1,0:T(8,128)S(1)} %get-tuple-element.21), channel_id=1, source_target_pairs={{0,64},{1,65},{2,66},{3,67},{64,0},{65,1},{66,2},{67,3},{16,80},{1... | collective-permute-start | bytes 196616 | tf_op jit(solution)/shard_map/ppermute | solution.py:46
  188.2 24.7 %collective-permute-start.32 = (f32[256,1024]{1,0:T(8,128)}, f32[256,1024]{1,0:T(8,128)S(1)}, u32[]{:S(2)}, u32[]{:S(2)}) collective-permute-start(f32[256,1024]{1,0:T(8,128)} %get-tuple-element.14), channel_id=1, source_target_pairs={{0,2},{1,3},{2,0},{3,1},{64,66},{65,67},{66,64},{67,65},{16,18},{1... | collective-permute-start | bytes 3145736 | tf_op jit(solution)/shard_map/ppermute | solution.py:46
  191.6 5.9 %collective-permute-start.33 = (f32[64,256]{1,0:T(8,128)S(1)}, f32[64,256]{1,0:T(8,128)S(1)}, u32[]{:S(2)}, u32[]{:S(2)}) collective-permute-start(f32[64,256]{1,0:T(8,128)S(1)} %add_add_fusion), channel_id=1, source_target_pairs={{0,16},{1,17},{2,18},{3,19},{64,80},{65,81},{66,82},{67,83},{16,32... | collective-permute-start | bytes 196616 | tf_op jit(solution)/shard_map/ppermute | solution.py:46
  192.0 6.3 %collective-permute-start.34 = (f32[64,256]{1,0:T(8,128)S(1)}, f32[64,256]{1,0:T(8,128)S(1)}, u32[]{:S(2)}, u32[]{:S(2)}) collective-permute-start(f32[64,256]{1,0:T(8,128)S(1)} %add_add_fusion), channel_id=1, source_target_pairs={{0,32},{1,33},{2,34},{3,35},{64,96},{65,97},{66,98},{67,99},{16,48... | collective-permute-start | bytes 196616 | tf_op jit(solution)/shard_map/ppermute | solution.py:46
  (20 other events, 278.8 us)

commit v3 on v2

v3 whole, which is shorter than its diff:
```python
import jax
import jax.numpy as jnp
from jax import lax
from jax.experimental import pallas as pl
from jax.experimental.pallas import tpu as pltpu
from jax.sharding import PartitionSpec as P


AXES = ("prow", "pcol")
TILE = 256


def number(x, y, z, core):
    return ((z >> 1) * 4 + y) * 16 + x * 4 + (z & 1) * 2 + core


def pairs(on=None, off=None):
    found = []
    for x in range(4):
        for y in range(4):
            for z in range(4):
                move = on if (y & 1) == (z & 1) else off
                if move is not None:
                    for core in range(2):
                        tx, ty, tz, tc = move(x, y, z, core)
                        found.append((number(x, y, z, core), number(tx % 4, ty % 4, tz % 4, tc)))
    return found


def shift(dy, dz):
    return lambda x, y, z, c: (x, y + dy, z + dz, c)


def both(move):
    return pairs(move, move)


X_UP = both(lambda x, y, z, c: (x + 1, y, z, c))
X_DOWN = both(lambda x, y, z, c: (x - 1, y, z, c))
CORE = both(lambda x, y, z, c: (x, y, z, 1 - c))
Y_BY = [None] + [both(shift(d, 0)) for d in (1, 2, 3)]
Z_FLIP = [None] + [both(lambda x, y, z, c, d=d: (x, y, z ^ d, c)) for d in (1, 2, 3)]


def send(array, route):
    return lax.ppermute(array, AXES, route)


def parts(value):
    high = value.astype(jnp.bfloat16)
    return high, (value - high.astype(jnp.float32)).astype(jnp.bfloat16)


def dot(a, b):
    return lax.dot_general(a, b, (((1,), (1,)), ((), ())), preferred_element_type=jnp.float32)


SLOTS = [
    ((0, -1), (-1, 2)),
    ((0, 1), (1, 2)),
    ((2, -1), (1, -1)),
    ((2, 1), (1, 1)),
    ((0, 0), (-1, 0)),
    ((2, 0), (1, 0)),
    ((0, 2), (-1, -1)),
    ((2, 2), (-1, 1)),
]


def slot_info(where, structure, entry, blocks):
    x, y, z, core = where[0], where[1], where[2], where[3]
    on = (y & 1) == (z & 1)
    ys = (y + jnp.where(on, entry[0][0], entry[1][0])) & 3
    zs = (z + jnp.where(on, entry[0][1], entry[1][1])) & 3
    block = (zs >> 1) * 4 + ys
    delta = ((block >> 1) - x) & 3
    place = jnp.where(delta == 0, 0, jnp.where(delta == 3, 1, delta + 1))
    supernode = x * 4 + (zs & 1) * 2 + core
    return place, (zs ^ z) & 1, [structure[supernode, block * blocks + b].astype(jnp.float32) for b in range(blocks)]


def multiply_kernel(where, structure, *refs):
    own, from_left, opposite, from_right, two_off, t0, w_top, w_bottom, t1, s0, s1, s2, s3, own_tile, s0_tile, s1_tile = refs[:16]
    pieces = refs[16:26]
    own_out, mate_top, mate_bottom, diag, high, low = refs[26:]
    rows, span = own.shape
    half = high.shape[2]
    blocks = span // rows
    step = pl.program_id(0)
    y, z, core = where[1], where[2], where[3]
    on = (y & 1) == (z & 1)

    @pl.when(step == 0)
    def _():
        def last(c):
            return jnp.where(on, jnp.concatenate([w_top[:, c], w_bottom[:, c]], axis=0), t1[:, c])

        def pick(a, b):
            return lambda c: jnp.where(on, a[:, c], b[:, c])

        values = [lambda c, ref=ref: ref[:, c] for ref in (s0, s1, s2, s3)]
        values += [pick(own, from_left), pick(opposite, from_right), pick(two_off, t0), last]
        for value, entry in zip(values, SLOTS):
            place, side, keeps = slot_info(where, structure, entry, blocks)
            row = pl.multiple_of(side * rows, rows)
            for b, keep in enumerate(keeps):
                hi, lo = parts(value(slice(b * rows, (b + 1) * rows)) * keep)
                g, inner = divmod(b * rows, half)
                at = place * 2 + (g ^ core)
                high[at, pl.ds(row, rows), inner : inner + rows] = hi
                low[at, pl.ds(row, rows), inner : inner + rows] = lo
        diag[...] = jnp.zeros(diag.shape, jnp.float32)

    first = step < pl.num_programs(0) // 2
    acc = jnp.zeros((2 * rows, TILE), jnp.float32)
    for j in range(8):
        if j < 6:
            value = pieces[j][...]
        else:
            value = jnp.where(first, pieces[2 * j - 6][...], pieces[2 * j - 5][...])
        a, b = parts(value)
        acc += dot(high[j], a) + dot(high[j], b) + dot(low[j], a)
    own_sum, mate_sum = acc[:rows], acc[rows:]
    own_out[...] = own_sum
    mate_top[...] = mate_sum[: rows // 2]
    mate_bottom[...] = mate_sum[rows // 2 :]

    column = ((z >> 1) * 4 + y) * blocks + step
    supernode = where[0] * 4 + (z & 1) * 2 + core
    keep_own = structure[supernode, column].astype(jnp.float32)
    keep_mate = structure[supernode ^ 2, column].astype(jnp.float32)
    panels = (own_tile[...] * keep_own, jnp.where((z & 1) == 1, s0_tile[...], s1_tile[...]) * keep_mate)
    for r, (result, panel) in enumerate(zip((own_sum, mate_sum), panels)):
        a, b = parts(result)
        c, d = parts(panel)
        diag[r] += dot(a, c) + dot(a, d) + dot(b, c)

    @pl.when(step == pl.num_programs(0) - 1)
    def _():
        total = diag[0]
        diag[0] = total + jnp.where(on, 0.0, total.T)
        diag[1] = jnp.where(on, diag[1], 0.0)


def multiply(where, structure, slots, tiles, pieces):
    rows, span = slots[0].shape
    half = span // 2
    middle = span // TILE // 2
    at_column = lambda height: pl.BlockSpec((height, TILE), lambda i, *_: (0, i))
    whole = lambda shape: pl.BlockSpec(shape, lambda i, *_: (0,) * len(shape))
    every = pl.BlockSpec((TILE, half), lambda i, *_: (i, 0))
    top = pl.BlockSpec((TILE, half), lambda i, *_: (jnp.minimum(i, middle - 1), 0))
    bottom = pl.BlockSpec((TILE, half), lambda i, *_: (jnp.maximum(i - middle, 0), 0))
    outs = [(rows, span), (rows // 2, span), (rows // 2, span), (2, rows, rows)]
    return pl.pallas_call(
        multiply_kernel,
        grid_spec=pltpu.PrefetchScalarGridSpec(
            num_scalar_prefetch=2,
            grid=(span // TILE,),
            in_specs=[whole(a.shape) for a in slots]
            + [at_column(rows)] * len(tiles)
            + [every] * 6
            + [top, bottom] * 2,
            out_specs=[at_column(shape[0]) for shape in outs[:3]] + [whole(outs[3])],
            scratch_shapes=[pltpu.VMEM((8, 2 * rows, half), jnp.bfloat16)] * 2,
        ),
        out_shape=[jax.ShapeDtypeStruct(shape, jnp.float32) for shape in outs],
        compiler_params=pltpu.CompilerParams(vmem_limit_bytes=60 * 2**20),
        cost_estimate=pl.CostEstimate(
            flops=48 * rows * span * span, bytes_accessed=4 * (rows * span * 16 + 4 * span * span), transcendentals=0
        ),
    )(where, structure, *slots, *tiles, *pieces)


def local(panel_t, ancestor, structure, diag_inv):
    width = panel_t.shape[1]
    span = panel_t.shape[2]
    prow = lax.axis_index("prow")
    pcol = lax.axis_index("pcol")
    x = pcol >> 2
    y = prow & 3
    z = (prow >> 2) * 2 + ((pcol >> 1) & 1)
    core = pcol & 1
    on = (y & 1) == (z & 1)
    own = panel_t.reshape(width, span)
    split = width // 2
    half = ancestor.shape[0] // 2

    from_left = send(own, both(shift(1, 0)))
    from_right = send(own, both(shift(-1, 0)))
    two_off = send(own, pairs(on=shift(0, 2)))
    opposite = jnp.concatenate(
        [send(from_left[:split], both(shift(1, 0))), send(from_right[split:], both(shift(-1, 0)))],
        axis=0,
    )
    turned = jnp.where(on, two_off, own)
    s0 = send(turned, pairs(on=shift(1, 0), off=shift(0, 1)))
    s1 = send(turned, pairs(on=shift(-1, 0), off=shift(0, -1)))
    t0 = send(from_left, pairs(on=shift(0, 1)))
    t1 = send(from_left, pairs(on=shift(0, -1)))
    crossed = jnp.where(on, from_right, opposite)
    s2 = send(crossed, pairs(on=shift(0, 1), off=shift(0, 1)))
    s3 = send(crossed, pairs(on=shift(0, -1), off=shift(0, -1)))
    w_top = send(s0[:split], pairs(off=shift(1, 0)))
    w_bottom = send(s1[split:], pairs(off=shift(-1, 0)))

    left = send(ancestor, X_UP)
    right = send(ancestor, X_DOWN)
    far = [send(left[:half], X_UP), send(right[half:], X_DOWN)]
    pieces = []
    for piece in (ancestor, left, right):
        pieces += [piece, send(piece, CORE)]
    pieces += far + [send(piece, CORE) for piece in far]

    where = jnp.stack([x, y, z, core]).astype(jnp.int32)
    slots = [own, from_left, opposite, from_right, two_off, t0, w_top, w_bottom, t1, s0, s1, s2, s3]
    own_out, mate_top, mate_bottom, partial = multiply(where, structure, slots, [own, s0, s1], pieces)
    received = jnp.concatenate([send(mate_top, Z_FLIP[1]), send(mate_bottom, Z_FLIP[1])], axis=0)

    quarter = width // 4
    cut = partial.reshape(2, 4, quarter, width)
    summed = lax.dynamic_index_in_dim(cut, y, 1, False)
    for d in (1, 2, 3):
        summed = summed + send(lax.dynamic_index_in_dim(cut, (y + d) & 3, 1, False), Y_BY[d])
    mine, mates = summed[0], summed[1]
    total = mine + send(mates, Z_FLIP[1]) + send(mine, Z_FLIP[2]) + send(mates, Z_FLIP[3])
    own_out, total = lax.optimization_barrier((own_out, total))
    diag = jnp.zeros((4, quarter, width), jnp.float32)
    diag = lax.dynamic_update_index_in_dim(diag, total, y, 0)
    for d in (1, 2, 3):
        diag = lax.dynamic_update_index_in_dim(diag, send(total, Y_BY[d]), (y - d) & 3, 0)
    return -(own_out + received), diag_inv + diag.reshape(1, width, width)


def solution(mesh):
    return jax.shard_map(
        local,
        mesh=mesh,
        in_specs=(P("pcol", None, "prow"), P("prow", "pcol"), P(), P("pcol", None, None)),
        out_specs=(P("pcol", "prow"), P("pcol", None, None)),
        check_vma=False,
    )
```

time: 215 us -> 216 us (level)
  Pallas kernels: 42.5 us -> 26.8 us
  waiting for transfers between devices: 108 us -> 123 us
  starting transfers between devices: 46.9 us -> 53 us
  local copies, waits for them, and re-layouts: 10.8 us -> 5.16 us
    pallas_call x2 -> x1, Pallas kernels: 42.5 us -> 26.8 us  [multiply(): pl.pallas_call(multiply_kernel, grid_spec=pltpu.PrefetchScalarGridSpec(nu...]
    ppermute x36 -> x33, waiting for transfers between devices: 108 us -> 123 us  [send(): return lax.ppermute(array, AXES, route)]
    ppermute x36 -> x33, starting transfers between devices: 46.9 us -> 53 us  [send(): return lax.ppermute(array, AXES, route)]
    unnamed x33 -> x29, local copies, waits for them, and re-layouts: 4.22 us -> 0.1 us
  transfers between devices with their start and end apart: 36 -> 33, of which waited for: 16 -> 18; matrix products, arithmetic and copies ran while one was open for 4% -> 3% of each run, Pallas kernels for 11% -> 0%
where the time goes in v3:
time: 216 us; the launch traced here: 214 us
  waiting for transfers between devices  123 us (57%)
  starting transfers between devices  53 us (25%)
  Pallas kernels  26.8 us (12%)
  other arithmetic  5.39 us (2%)
  local copies, waits for them, and re-layouts  5.16 us (2%)
    ppermute x33, waiting for transfers between devices, send(): return lax.ppermute(array, AXES, route)  123 us
    ppermute x33, starting transfers between devices, send(): return lax.ppermute(array, AXES, route)  53 us
    pallas_call x1, Pallas kernels, multiply(): pl.pallas_call(multiply_kernel, grid_spec=pltpu.PrefetchScalarGridSpec(nu...  26.8 us
  transfers between devices with their start and end apart: 33, of which 18 were waited for; matrix products, arithmetic and copies ran while one was open for 3% of the time, Pallas kernels for 0%

profile of v3, /device:TPU:32, one launch (start us, length us, event | category | flops | bytes accessed | tf_op | source)
XLA Modules:
  0.0 214.1 jit_solution(8071060843545386254)
XLA Ops:
  0.6 1.6 collective-permute-start
  3.0 1.6 collective-permute-start.14
  4.6 5.8 %collective-permute-start.2 = (f32[256,1024]{1,0:T(8,128)}, f32[256,1024]{1,0:T(8,128)S(1)}, u32[]{:S(2)}, u32[]{:S(2)}) collective-permute-start(f32[256,1024]{1,0:T(8,128)} %bitcast.39), channel_id=1, source_target_pairs={{0,48},{1,49},{2,50},{3,51},{64,112},{65,113},{66,114},{67,115},{1... | collective-permute-start | bytes 3145736 | tf_op jit(solution)/shard_map/ppermute | solution.py:46
  10.4 1.7 collective-permute-start.16
  12.1 15.1 %collective-permute-done.refs_1_ = f32[256,1024]{1,0:T(8,128)} collective-permute-done((f32[256,1024]{1,0:T(8,128)}, f32[256,1024]{1,0:T(8,128)}, u32[]{:S(2)}, u32[]{:S(2)}) %collective-permute-start) | collective-permute-done | bytes 1048608 | tf_op jit(solution)/shard_map/ppermute | solution.py:46
  28.6 1.7 broadcast_select_fusion.1
  30.4 3.8 %collective-permute-start.6 = (f32[256,1024]{1,0:T(8,128)S(1)}, f32[256,1024]{1,0:T(8,128)S(1)}, u32[]{:S(2)}, u32[]{:S(2)}) collective-permute-start(f32[256,1024]{1,0:T(8,128)S(1)} %broadcast_select_fusion.1), channel_id=1, source_target_pairs={{0,16},{1,17},{2,64},{3,65},{64,80},{65,81},{66,0},{67,1},{16,18},... | collective-permute-start | bytes 3145736 | tf_op jit(solution)/shard_map/ppermute | solution.py:46
  34.4 10.0 %collective-permute-done.1 = f32[128,1024]{1,0:T(8,128)S(1)} collective-permute-done((f32[128,1024]{1,0:T(8,128)S(1)}, f32[128,1024]{1,0:T(8,128)S(1)}, u32[]{:S(2)}, u32[]{:S(2)}) %collective-permute-start.1) | collective-permute-done | bytes 524320 | tf_op jit(solution)/shard_map/ppermute | solution.py:46
  44.4 11.9 %collective-permute-done.3 = f32[128,1024]{1,0:T(8,128)S(1)} collective-permute-done((f32[128,1024]{1,0:T(8,128)S(1)}, f32[128,1024]{1,0:T(8,128)S(1)}, u32[]{:S(2)}, u32[]{:S(2)}) %collective-permute-start.3) | collective-permute-done | bytes 524320 | tf_op jit(solution)/shard_map/ppermute | solution.py:46
  56.4 8.5 %collective-permute-done.6.refs_9_.refs_14_ = f32[256,1024]{1,0:T(8,128)S(1)} collective-permute-done((f32[256,1024]{1,0:T(8,128)S(1)}, f32[256,1024]{1,0:T(8,128)S(1)}, u32[]{:S(2)}, u32[]{:S(2)}) %collective-permute-start.6) | collective-permute-done | bytes 1048608 | tf_op jit(solution)/shard_map/ppermute | solution.py:46
  67.7 4.3 %collective-permute-start.11 = (f32[256,1024]{1,0:T(8,128)S(1)}, f32[256,1024]{1,0:T(8,128)S(1)}, u32[]{:S(2)}, u32[]{:S(2)}) collective-permute-start(f32[256,1024]{1,0:T(8,128)S(1)} %broadcast_select_fusion), channel_id=1, source_target_pairs={{0,2},{1,3},{2,64},{3,65},{64,66},{65,67},{66,0},{67,1},{16,18},{1... | collective-permute-start | bytes 3145736 | tf_op jit(solution)/shard_map/ppermute | solution.py:46
  74.6 2.4 %collective-permute-done.8.refs_10_.refs_15_ = f32[256,1024]{1,0:T(8,128)S(1)} collective-permute-done((f32[256,1024]{1,0:T(8,128)S(1)}, f32[256,1024]{1,0:T(8,128)S(1)}, u32[]{:S(2)}, u32[]{:S(2)}) %collective-permute-start.8) | collective-permute-done | bytes 1048608 | tf_op jit(solution)/shard_map/ppermute | solution.py:46
  77.0 2.3 %collective-permute-start.12 = (f32[256,1024]{1,0:T(8,128)S(1)}, f32[256,1024]{1,0:T(8,128)S(1)}, u32[]{:S(2)}, u32[]{:S(2)}) collective-permute-start(f32[256,1024]{1,0:T(8,128)S(1)} %broadcast_select_fusion), channel_id=1, source_target_pairs={{0,66},{1,67},{2,0},{3,1},{64,2},{65,3},{66,64},{67,65},{16,82},{1... | collective-permute-start | bytes 3145736 | tf_op jit(solution)/shard_map/ppermute | solution.py:46
  79.3 13.7 %collective-permute-done.10.refs_8_ = f32[256,1024]{1,0:T(8,128)S(1)} collective-permute-done((f32[256,1024]{1,0:T(8,128)}, f32[256,1024]{1,0:T(8,128)S(1)}, u32[]{:S(2)}, u32[]{:S(2)}) %collective-permute-start.10) | collective-permute-done | bytes 1048608 | tf_op jit(solution)/shard_map/ppermute | solution.py:46
  93.0 1.5 collective-permute-start.18
  94.5 2.0 collective-permute-done.5.refs_5_
  96.5 2.8 %collective-permute-start.19 = (f32[512,512]{1,0:T(8,128)S(1)}, f32[512,512]{1,0:T(8,128)}, u32[]{:S(2)}, u32[]{:S(2)}) collective-permute-start(f32[512,512]{1,0:T(8,128)S(1)} %slice.37), channel_id=1, source_target_pairs={{0,12},{1,13},{2,14},{3,15},{64,76},{65,77},{66,78},{67,79},{16,28... | collective-permute-start | bytes 3145736 | tf_op jit(solution)/shard_map/ppermute | solution.py:46
  99.3 16.9 %collective-permute-done.11.refs_11_ = f32[256,1024]{1,0:T(8,128)S(1)} collective-permute-done((f32[256,1024]{1,0:T(8,128)S(1)}, f32[256,1024]{1,0:T(8,128)S(1)}, u32[]{:S(2)}, u32[]{:S(2)}) %collective-permute-start.11) | collective-permute-done | bytes 1048608 | tf_op jit(solution)/shard_map/ppermute | solution.py:46
  118.4 11.3 %collective-permute-done.7.refs_6_ = f32[128,1024]{1,0:T(8,128)S(1)} collective-permute-done((f32[128,1024]{1,0:T(8,128)S(1)}, f32[128,1024]{1,0:T(8,128)S(1)}, u32[]{:S(2)}, u32[]{:S(2)}) %collective-permute-start.7) | collective-permute-done | bytes 524320 | tf_op jit(solution)/shard_map/ppermute | solution.py:46
  129.7 4.3 %collective-permute-start.9 = (f32[128,1024]{1,0:T(8,128)S(1)}, f32[128,1024]{1,0:T(8,128)}, u32[]{:S(2)}, u32[]{:S(2)}) collective-permute-start(f32[128,1024]{1,0:T(8,128)S(1)} %slice.35), channel_id=1, source_target_pairs={{2,50},{3,51},{66,114},{67,115},{16,0},{17,1},{80,64},{81,65},{34,... | collective-permute-start | bytes 1572872 | tf_op jit(solution)/shard_map/ppermute | solution.py:46
  134.7 9.8 %collective-permute-done.9.refs_7_ = f32[128,1024]{1,0:T(8,128)} collective-permute-done((f32[128,1024]{1,0:T(8,128)S(1)}, f32[128,1024]{1,0:T(8,128)}, u32[]{:S(2)}, u32[]{:S(2)}) %collective-permute-start.9) | collective-permute-done | bytes 524320 | tf_op jit(solution)/shard_map/ppermute | solution.py:46
  144.5 26.8 %shard_map.59 = (f32[256,1024]{1,0:T(8,128)}, f32[128,1024]{1,0:T(8,128)}, f32[128,1024]{1,0:T(8,128)}, f32[2,256,256]{2,1,0:T(8,128)}) custom-call(s32[4]{0:T(128)} %pad_add_fusion.where, s32[16,32]{1,0:T(8,128)} %structure.1, f32[256,1024]{1,0:T(8,128)} %bitcast.40, f32[256,1024]{1,0:T(8,128)} %collective-permute-done.refs_1_, f32[256,1024]{1,0:T(8,128)} %copy-done.1, ...), custom_call_target="tpu_custom_call" | custom-call | flops 12884901888 | bytes 33554432 | tf_op jit(solution)/shard_map/pallas_call | solution.py:155
  172.5 3.5 %collective-permute-start.22 = (f32[2,64,256]{2,1,0:T(8,128)S(1)}, f32[2,64,256]{2,1,0:T(8,128)S(1)}, u32[]{:S(2)}, u32[]{:S(2)}) collective-permute-start(f32[2,64,256]{2,1,0:T(8,128)S(1)} %get-tuple-element.14), channel_id=1, source_target_pairs={{0,16},{1,17},{2,18},{3,19},{64,80},{65,81},{66,82},{67,83},{16,32... | collective-permute-start | bytes 393224 | tf_op jit(solution)/shard_map/ppermute | solution.py:46
  176.0 1.8 collective-permute-start.23
  180.1 3.0 %collective-permute-done.23 = f32[2,64,256]{2,1,0:T(8,128)S(1)} collective-permute-done((f32[2,64,256]{2,1,0:T(8,128)S(1)}, f32[2,64,256]{2,1,0:T(8,128)S(1)}, u32[]{:S(2)}, u32[]{:S(2)}) %collective-permute-start.23) | collective-permute-done | bytes 131104 | tf_op jit(solution)/shard_map/ppermute | solution.py:46
  184.1 2.6 %collective-permute-start.25 = (f32[64,256]{1,0:T(8,128)S(1)}, f32[64,256]{1,0:T(8,128)S(1)}, u32[]{:S(2)}, u32[]{:S(2)}) collective-permute-start(f32[64,256]{1,0:T(8,128)S(1)} %get-tuple-element.18), channel_id=1, source_target_pairs={{0,2},{1,3},{2,0},{3,1},{64,66},{65,67},{66,64},{67,65},{16,18},{1... | collective-permute-start | bytes 196616 | tf_op jit(solution)/shard_map/ppermute | solution.py:46
  188.3 3.1 %collective-permute-start.28 = (f32[128,1024]{1,0:T(8,128)}, f32[128,1024]{1,0:T(8,128)S(1)}, u32[]{:S(2)}, u32[]{:S(2)}) collective-permute-start(f32[128,1024]{1,0:T(8,128)} %get-tuple-element.11), channel_id=1, source_target_pairs={{0,2},{1,3},{2,0},{3,1},{64,66},{65,67},{66,64},{67,65},{16,18},{1... | collective-permute-start | bytes 1572872 | tf_op jit(solution)/shard_map/ppermute | solution.py:46
  191.5 1.7 collective-permute-done.26
  193.6 3.5 %collective-permute-start.31 = (f32[64,256]{1,0:T(8,128)S(1)}, f32[64,256]{1,0:T(8,128)S(1)}, u32[]{:S(2)}, u32[]{:S(2)}) collective-permute-start(f32[64,256]{1,0:T(8,128)S(1)} %add_add_fusion), channel_id=1, source_target_pairs={{0,32},{1,33},{2,34},{3,35},{64,96},{65,97},{66,98},{67,99},{16,48... | collective-permute-start | bytes 196616 | tf_op jit(solution)/shard_map/ppermute | solution.py:46
  197.1 1.6 collective-permute-done.30
  202.1 2.3 %collective-permute-done.28 = f32[128,1024]{1,0:T(8,128)S(1)} collective-permute-done((f32[128,1024]{1,0:T(8,128)}, f32[128,1024]{1,0:T(8,128)S(1)}, u32[]{:S(2)}, u32[]{:S(2)}) %collective-permute-start.28) | collective-permute-done | bytes 524320 | tf_op jit(solution)/shard_map/ppermute | solution.py:46
  204.4 8.5 %collective-permute-done.29 = f32[128,1024]{1,0:T(8,128)S(1)} collective-permute-done((f32[128,1024]{1,0:T(8,128)}, f32[128,1024]{1,0:T(8,128)S(1)}, u32[]{:S(2)}, u32[]{:S(2)}) %collective-permute-start.29) | collective-permute-done | bytes 524320 | tf_op jit(solution)/shard_map/ppermute | solution.py:46
  (85 shorter events, 21.4 us)
Async XLA Ops:
  0.6 26.6 %collective-permute-start = (f32[256,1024]{1,0:T(8,128)}, f32[256,1024]{1,0:T(8,128)}, u32[]{:S(2)}, u32[]{:S(2)}) collective-permute-start(f32[256,1024]{1,0:T(8,128)} %bitcast.37), channel_id=1, source_target_pairs={{0,16},{1,17},{2,18},{3,19},{64,80},{65,81},{66,82},{67,83},{16,32... | collective-permute-start | bytes 3145736 | tf_op jit(solution)/shard_map/ppermute | solution.py:46
  2.3 26.4 %collective-permute-start.4 = (f32[256,1024]{1,0:T(8,128)}, f32[256,1024]{1,0:T(8,128)S(1)}, u32[]{:S(2)}, u32[]{:S(2)}) collective-permute-start(f32[256,1024]{1,0:T(8,128)} %bitcast.38), channel_id=1, source_target_pairs={{0,64},{1,65},{64,0},{65,1},{18,82},{19,83},{82,18},{83,19},{32,96... | collective-permute-start | bytes 3145736 | tf_op jit(solution)/shard_map/ppermute | solution.py:46
  3.0 63.2 %collective-permute-start.14 = (f32[1024,512]{1,0:T(8,128)}, f32[1024,512]{1,0:T(8,128)}, u32[]{:S(2)}, u32[]{:S(2)}) collective-permute-start(f32[1024,512]{1,0:T(8,128)} %refs_16_.1), channel_id=1, source_target_pairs={{0,4},{1,5},{2,6},{3,7},{64,68},{65,69},{66,70},{67,71},{16,20},{1... | collective-permute-start | bytes 6291464 | tf_op jit(solution)/shard_map/ppermute | solution.py:46
  4.6 29.7 %collective-permute-start.2 = (f32[256,1024]{1,0:T(8,128)}, f32[256,1024]{1,0:T(8,128)S(1)}, u32[]{:S(2)}, u32[]{:S(2)}) collective-permute-start(f32[256,1024]{1,0:T(8,128)} %bitcast.39), channel_id=1, source_target_pairs={{0,48},{1,49},{2,50},{3,51},{64,112},{65,113},{66,114},{67,115},{1... | collective-permute-start | bytes 3145736 | tf_op jit(solution)/shard_map/ppermute | solution.py:46
  10.4 57.3 %collective-permute-start.16 = (f32[1024,512]{1,0:T(8,128)}, f32[1024,512]{1,0:T(8,128)}, u32[]{:S(2)}, u32[]{:S(2)}) collective-permute-start(f32[1024,512]{1,0:T(8,128)} %refs_16_.1), channel_id=1, source_target_pairs={{0,12},{1,13},{2,14},{3,15},{64,76},{65,77},{66,78},{67,79},{16,28... | collective-permute-start | bytes 6291464 | tf_op jit(solution)/shard_map/ppermute | solution.py:46
  28.3 16.1 %collective-permute-start.1 = (f32[128,1024]{1,0:T(8,128)S(1)}, f32[128,1024]{1,0:T(8,128)S(1)}, u32[]{:S(2)}, u32[]{:S(2)}) collective-permute-start(f32[128,1024]{1,0:T(8,128)S(1)} %slice.32), channel_id=1, source_target_pairs={{0,16},{1,17},{2,18},{3,19},{64,80},{65,81},{66,82},{67,83},{16,32... | collective-permute-start | bytes 1572872 | tf_op jit(solution)/shard_map/ppermute | solution.py:46
  30.4 34.5 %collective-permute-start.6 = (f32[256,1024]{1,0:T(8,128)S(1)}, f32[256,1024]{1,0:T(8,128)S(1)}, u32[]{:S(2)}, u32[]{:S(2)}) collective-permute-start(f32[256,1024]{1,0:T(8,128)S(1)} %broadcast_select_fusion.1), channel_id=1, source_target_pairs={{0,16},{1,17},{2,64},{3,65},{64,80},{65,81},{66,0},{67,1},{16,18},... | collective-permute-start | bytes 3145736 | tf_op jit(solution)/shard_map/ppermute | solution.py:46
  34.2 65.0 %collective-permute-start.13 = (f32[1024,512]{1,0:T(8,128)S(1)}, f32[1024,512]{1,0:T(8,128)S(1)}, u32[]{:S(2)}, u32[]{:S(2)}) collective-permute-start(f32[1024,512]{1,0:T(8,128)S(1)} %copy-done.7), channel_id=1, source_target_pairs={{0,1},{1,0},{2,3},{3,2},{64,65},{65,64},{66,67},{67,66},{16,17},{1... | collective-permute-start | bytes 6291464 | tf_op jit(solution)/shard_map/ppermute | solution.py:46
  44.3 12.0 %collective-permute-start.3 = (f32[128,1024]{1,0:T(8,128)S(1)}, f32[128,1024]{1,0:T(8,128)S(1)}, u32[]{:S(2)}, u32[]{:S(2)}) collective-permute-start(f32[128,1024]{1,0:T(8,128)S(1)} %slice.33), channel_id=1, source_target_pairs={{0,48},{1,49},{2,50},{3,51},{64,112},{65,113},{66,114},{67,115},{1... | collective-permute-start | bytes 1572872 | tf_op jit(solution)/shard_map/ppermute | solution.py:46
  56.3 20.7 %collective-permute-start.8 = (f32[256,1024]{1,0:T(8,128)S(1)}, f32[256,1024]{1,0:T(8,128)S(1)}, u32[]{:S(2)}, u32[]{:S(2)}) collective-permute-start(f32[256,1024]{1,0:T(8,128)S(1)} %broadcast_select_fusion.1), channel_id=1, source_target_pairs={{0,48},{1,49},{2,0},{3,1},{64,112},{65,113},{66,64},{67,65},{16,82... | collective-permute-start | bytes 3145736 | tf_op jit(solution)/shard_map/ppermute | solution.py:46
  64.9 28.1 %collective-permute-start.10 = (f32[256,1024]{1,0:T(8,128)}, f32[256,1024]{1,0:T(8,128)S(1)}, u32[]{:S(2)}, u32[]{:S(2)}) collective-permute-start(f32[256,1024]{1,0:T(8,128)} %collective-permute-done.refs_1_), channel_id=1, source_target_pairs={{0,66},{1,67},{64,2},{65,3},{18,16},{19,17},{82,80},{83,81},{32,98... | collective-permute-start | bytes 3145736 | tf_op jit(solution)/shard_map/ppermute | solution.py:46
  66.2 30.3 %collective-permute-start.5 = (f32[256,1024]{1,0:T(8,128)}, f32[256,1024]{1,0:T(8,128)S(1)}, u32[]{:S(2)}, u32[]{:S(2)}) collective-permute-start(f32[256,1024]{1,0:T(8,128)} %collective-permute-done.refs_1_), channel_id=1, source_target_pairs={{0,2},{1,3},{64,66},{65,67},{18,80},{19,81},{82,16},{83,17},{32,34... | collective-permute-start | bytes 3145736 | tf_op jit(solution)/shard_map/ppermute | solution.py:46
  67.7 48.5 %collective-permute-start.11 = (f32[256,1024]{1,0:T(8,128)S(1)}, f32[256,1024]{1,0:T(8,128)S(1)}, u32[]{:S(2)}, u32[]{:S(2)}) collective-permute-start(f32[256,1024]{1,0:T(8,128)S(1)} %broadcast_select_fusion), channel_id=1, source_target_pairs={{0,2},{1,3},{2,64},{3,65},{64,66},{65,67},{66,0},{67,1},{16,18},{1... | collective-permute-start | bytes 3145736 | tf_op jit(solution)/shard_map/ppermute | solution.py:46
  77.0 39.2 %collective-permute-start.12 = (f32[256,1024]{1,0:T(8,128)S(1)}, f32[256,1024]{1,0:T(8,128)S(1)}, u32[]{:S(2)}, u32[]{:S(2)}) collective-permute-start(f32[256,1024]{1,0:T(8,128)S(1)} %broadcast_select_fusion), channel_id=1, source_target_pairs={{0,66},{1,67},{2,0},{3,1},{64,2},{65,3},{66,64},{67,65},{16,82},{1... | collective-permute-start | bytes 3145736 | tf_op jit(solution)/shard_map/ppermute | solution.py:46
  93.0 24.6 %collective-permute-start.18 = (f32[512,512]{1,0:T(8,128)S(1)}, f32[512,512]{1,0:T(8,128)}, u32[]{:S(2)}, u32[]{:S(2)}) collective-permute-start(f32[512,512]{1,0:T(8,128)S(1)} %slice.36), channel_id=1, source_target_pairs={{0,4},{1,5},{2,6},{3,7},{64,68},{65,69},{66,70},{67,71},{16,20},{1... | collective-permute-start | bytes 3145736 | tf_op jit(solution)/shard_map/ppermute | solution.py:46
  96.5 21.7 %collective-permute-start.19 = (f32[512,512]{1,0:T(8,128)S(1)}, f32[512,512]{1,0:T(8,128)}, u32[]{:S(2)}, u32[]{:S(2)}) collective-permute-start(f32[512,512]{1,0:T(8,128)S(1)} %slice.37), channel_id=1, source_target_pairs={{0,12},{1,13},{2,14},{3,15},{64,76},{65,77},{66,78},{67,79},{16,28... | collective-permute-start | bytes 3145736 | tf_op jit(solution)/shard_map/ppermute | solution.py:46
  99.3 45.2 %collective-permute-start.15 = (f32[1024,512]{1,0:T(8,128)}, f32[1024,512]{1,0:T(8,128)}, u32[]{:S(2)}, u32[]{:S(2)}) collective-permute-start(f32[1024,512]{1,0:T(8,128)} %collective-permute-done.14.refs_18_), channel_id=1, source_target_pairs={{0,1},{1,0},{2,3},{3,2},{64,65},{65,64},{66,67},{67,66},{16,17},{1... | collective-permute-start | bytes 6291464 | tf_op jit(solution)/shard_map/ppermute | solution.py:46
  116.2 28.3 %collective-permute-start.17 = (f32[1024,512]{1,0:T(8,128)}, f32[1024,512]{1,0:T(8,128)}, u32[]{:S(2)}, u32[]{:S(2)}) collective-permute-start(f32[1024,512]{1,0:T(8,128)} %collective-permute-done.16.refs_20_), channel_id=1, source_target_pairs={{0,1},{1,0},{2,3},{3,2},{64,65},{65,64},{66,67},{67,66},{16,17},{1... | collective-permute-start | bytes 6291464 | tf_op jit(solution)/shard_map/ppermute | solution.py:46
  116.3 13.4 %collective-permute-start.7 = (f32[128,1024]{1,0:T(8,128)S(1)}, f32[128,1024]{1,0:T(8,128)S(1)}, u32[]{:S(2)}, u32[]{:S(2)}) collective-permute-start(f32[128,1024]{1,0:T(8,128)S(1)} %slice.34), channel_id=1, source_target_pairs={{2,18},{3,19},{66,82},{67,83},{16,32},{17,33},{80,96},{81,97},{34,... | collective-permute-start | bytes 1572872 | tf_op jit(solution)/shard_map/ppermute | solution.py:46
  117.6 26.9 %collective-permute-start.20 = (f32[512,512]{1,0:T(8,128)}, f32[512,512]{1,0:T(8,128)}, u32[]{:S(2)}, u32[]{:S(2)}) collective-permute-start(f32[512,512]{1,0:T(8,128)} %collective-permute-done.18.refs_22_), channel_id=1, source_target_pairs={{0,1},{1,0},{2,3},{3,2},{64,65},{65,64},{66,67},{67,66},{16,17},{1... | collective-permute-start | bytes 3145736 | tf_op jit(solution)/shard_map/ppermute | solution.py:46
  118.2 26.3 %collective-permute-start.21 = (f32[512,512]{1,0:T(8,128)}, f32[512,512]{1,0:T(8,128)}, u32[]{:S(2)}, u32[]{:S(2)}) collective-permute-start(f32[512,512]{1,0:T(8,128)} %collective-permute-done.19.refs_23_), channel_id=1, source_target_pairs={{0,1},{1,0},{2,3},{3,2},{64,65},{65,64},{66,67},{67,66},{16,17},{1... | collective-permute-start | bytes 3145736 | tf_op jit(solution)/shard_map/ppermute | solution.py:46
  129.7 14.8 %collective-permute-start.9 = (f32[128,1024]{1,0:T(8,128)S(1)}, f32[128,1024]{1,0:T(8,128)}, u32[]{:S(2)}, u32[]{:S(2)}) collective-permute-start(f32[128,1024]{1,0:T(8,128)S(1)} %slice.35), channel_id=1, source_target_pairs={{2,50},{3,51},{66,114},{67,115},{16,0},{17,1},{80,64},{81,65},{34,... | collective-permute-start | bytes 1572872 | tf_op jit(solution)/shard_map/ppermute | solution.py:46
  172.5 7.6 %collective-permute-start.22 = (f32[2,64,256]{2,1,0:T(8,128)S(1)}, f32[2,64,256]{2,1,0:T(8,128)S(1)}, u32[]{:S(2)}, u32[]{:S(2)}) collective-permute-start(f32[2,64,256]{2,1,0:T(8,128)S(1)} %get-tuple-element.14), channel_id=1, source_target_pairs={{0,16},{1,17},{2,18},{3,19},{64,80},{65,81},{66,82},{67,83},{16,32... | collective-permute-start | bytes 393224 | tf_op jit(solution)/shard_map/ppermute | solution.py:46
  176.0 7.1 %collective-permute-start.23 = (f32[2,64,256]{2,1,0:T(8,128)S(1)}, f32[2,64,256]{2,1,0:T(8,128)S(1)}, u32[]{:S(2)}, u32[]{:S(2)}) collective-permute-start(f32[2,64,256]{2,1,0:T(8,128)S(1)} %get-tuple-element.16), channel_id=1, source_target_pairs={{0,32},{1,33},{2,34},{3,35},{64,96},{65,97},{66,98},{67,99},{16,48... | collective-permute-start | bytes 393224 | tf_op jit(solution)/shard_map/ppermute | solution.py:46
  177.8 5.3 %collective-permute-start.24 = (f32[2,64,256]{2,1,0:T(8,128)S(1)}, f32[2,64,256]{2,1,0:T(8,128)S(1)}, u32[]{:S(2)}, u32[]{:S(2)}) collective-permute-start(f32[2,64,256]{2,1,0:T(8,128)S(1)} %get-tuple-element.15), channel_id=1, source_target_pairs={{0,48},{1,49},{2,50},{3,51},{64,112},{65,113},{66,114},{67,115},{1... | collective-permute-start | bytes 393224 | tf_op jit(solution)/shard_map/ppermute | solution.py:46
  184.1 7.4 %collective-permute-start.25 = (f32[64,256]{1,0:T(8,128)S(1)}, f32[64,256]{1,0:T(8,128)S(1)}, u32[]{:S(2)}, u32[]{:S(2)}) collective-permute-start(f32[64,256]{1,0:T(8,128)S(1)} %get-tuple-element.18), channel_id=1, source_target_pairs={{0,2},{1,3},{2,0},{3,1},{64,66},{65,67},{66,64},{67,65},{16,18},{1... | collective-permute-start | bytes 196616 | tf_op jit(solution)/shard_map/ppermute | solution.py:46
  186.7 6.5 %collective-permute-start.26 = (f32[64,256]{1,0:T(8,128)S(1)}, f32[64,256]{1,0:T(8,128)S(1)}, u32[]{:S(2)}, u32[]{:S(2)}) collective-permute-start(f32[64,256]{1,0:T(8,128)S(1)} %get-tuple-element.17), channel_id=1, source_target_pairs={{0,64},{1,65},{2,66},{3,67},{64,0},{65,1},{66,2},{67,3},{16,80},{1... | collective-permute-start | bytes 196616 | tf_op jit(solution)/shard_map/ppermute | solution.py:46
  187.5 5.7 %collective-permute-start.27 = (f32[64,256]{1,0:T(8,128)S(1)}, f32[64,256]{1,0:T(8,128)S(1)}, u32[]{:S(2)}, u32[]{:S(2)}) collective-permute-start(f32[64,256]{1,0:T(8,128)S(1)} %get-tuple-element.18), channel_id=1, source_target_pairs={{0,66},{1,67},{2,64},{3,65},{64,2},{65,3},{66,0},{67,1},{16,82},{1... | collective-permute-start | bytes 196616 | tf_op jit(solution)/shard_map/ppermute | solution.py:46
  188.3 16.1 %collective-permute-start.28 = (f32[128,1024]{1,0:T(8,128)}, f32[128,1024]{1,0:T(8,128)S(1)}, u32[]{:S(2)}, u32[]{:S(2)}) collective-permute-start(f32[128,1024]{1,0:T(8,128)} %get-tuple-element.11), channel_id=1, source_target_pairs={{0,2},{1,3},{2,0},{3,1},{64,66},{65,67},{66,64},{67,65},{16,18},{1... | collective-permute-start | bytes 1572872 | tf_op jit(solution)/shard_map/ppermute | solution.py:46
  191.4 21.5 %collective-permute-start.29 = (f32[128,1024]{1,0:T(8,128)}, f32[128,1024]{1,0:T(8,128)S(1)}, u32[]{:S(2)}, u32[]{:S(2)}) collective-permute-start(f32[128,1024]{1,0:T(8,128)} %get-tuple-element.12), channel_id=1, source_target_pairs={{0,2},{1,3},{2,0},{3,1},{64,66},{65,67},{66,64},{67,65},{16,18},{1... | collective-permute-start | bytes 1572872 | tf_op jit(solution)/shard_map/ppermute | solution.py:46
  193.2 5.5 %collective-permute-start.30 = (f32[64,256]{1,0:T(8,128)S(1)}, f32[64,256]{1,0:T(8,128)S(1)}, u32[]{:S(2)}, u32[]{:S(2)}) collective-permute-start(f32[64,256]{1,0:T(8,128)S(1)} %add_add_fusion), channel_id=1, source_target_pairs={{0,16},{1,17},{2,18},{3,19},{64,80},{65,81},{66,82},{67,83},{16,32... | collective-permute-start | bytes 196616 | tf_op jit(solution)/shard_map/ppermute | solution.py:46
  193.6 6.4 %collective-permute-start.31 = (f32[64,256]{1,0:T(8,128)S(1)}, f32[64,256]{1,0:T(8,128)S(1)}, u32[]{:S(2)}, u32[]{:S(2)}) collective-permute-start(f32[64,256]{1,0:T(8,128)S(1)} %add_add_fusion), channel_id=1, source_target_pairs={{0,32},{1,33},{2,34},{3,35},{64,96},{65,97},{66,98},{67,99},{16,48... | collective-permute-start | bytes 196616 | tf_op jit(solution)/shard_map/ppermute | solution.py:46
  (15 other events, 429.8 us)
